TPU v7x, 32 devices: a whole 2x2x4 slice. The times are simulated.
32 devices in a mesh: orb: 8 (over z, core), grp: 4 (over y, x).
Axes of the slice: x: 2, y: 2, z: 4, core: 2. Of those that a mesh axis runs over, the one named last changes fastest.
Arguments:
- orbitals: bfloat16 [512, 32, 1024], P('orb', 'grp'), may hold values from -6 to 6
- pair_list: int32 [8, 8, 3], replicated, may hold values from 0 to 63, as said below
- offsets: int32 [512, 3], replicated, may hold values from 0 to 15
Outputs:
- exchange_action: float32 [512, 32, 1024], P('orb', 'grp')
Inputs may be any that keep to these rules, and one draw needn't show every extreme that they name: pair_list[o, r, 0] and pair_list[o, r, 1] are below 64; pair_list[o, r, 2] is a slot below 16, distinct within each block o, so a block names each owner group at most 2 times; in every draw some owner group is named 2 times by every block; the two orbitals of a pair differ.
All inputs are finite; a program needn't handle non-finite values.
Results may differ from a plain program's by a relative error of at most 0.0006.
Values may be sent and summed in bfloat16 or wider, within the bound.
A program may use at most 64 MiB of HBM per device.

v0:
```python
import math

import jax
import jax.numpy as jnp
import ml_dtypes
import numpy as np
from jax import lax
from jax.experimental import pallas as pl
from jax.experimental.pallas import tpu as pltpu
from jax.sharding import PartitionSpec as P

BOX = 32
ORB_GRP = 64
CAP = 2


screen_shift = 0.25
F32 = jnp.float32
BF16 = jnp.bfloat16


def split_table(table):
    wide = np.asarray(table, np.float32)
    high = wide.astype(ml_dtypes.bfloat16)
    low = (wide - high.astype(np.float32)).astype(ml_dtypes.bfloat16)
    return high, low


def fixed_tables(length):
    counts = np.arange(length) + 1.0
    sine = np.sqrt(2.0 / (length + 1.0)) * np.sin(
        math.pi * counts[:, None] * counts[None, :] / (length + 1.0)
    )
    levels = 2.0 - 2.0 * np.cos(math.pi * counts / (length + 1.0))
    green = 1.0 / (
        levels[:, None, None] + levels[None, :, None] + levels[None, None, :] + screen_shift
    )
    ones = np.ones((1, length))
    return (
        np.kron(sine, ones).astype(np.float32),
        np.kron(ones, sine).astype(np.float32),
        *split_table(sine),
        green.reshape(length, length * length).astype(np.float32),
    )


def split_field(field):
    high = field.astype(BF16)
    return high, (field - high.astype(F32)).astype(BF16)


def dot(left, right):
    return jnp.dot(left, right, preferred_element_type=F32)


def pair_kernel(
    moves, boxes, outer, inner, sine_high, sine_low, green, out, shifts, fields, plane_high, plane_low
):
    length, cells = green.shape
    share = boxes.shape[0] // 2
    row = lax.broadcasted_iota(jnp.int32, (length, cells), 0)
    col = lax.broadcasted_iota(jnp.int32, (length, cells), 1)
    mid = col // length
    last = col - mid * length

    def shift(field, dx, dy, dz):
        moved = pltpu.roll(field, jnp.remainder(-dx + length, length), 0)
        flat = jnp.remainder(2 * cells - dy * length - dz, cells)
        moved = pltpu.roll(moved, flat, 1)
        x, y, z = row + dx, mid + dy, last + dz
        keep = (x >= 0) & (x < length) & (y >= 0) & (y < length) & (z >= 0) & (z < length)
        return jnp.where(keep, moved, 0.0)

    def along_plane():
        high, low = split_field(fields[...])
        fields[...] = (
            dot(high, plane_high[...]) + dot(low, plane_high[...]) + dot(high, plane_low[...])
        )

    def along_x(field):
        high, low = split_field(field)
        return dot(sine_high[...], high) + dot(sine_high[...], low) + dot(sine_low[...], high)

    @pl.loop(0, length)
    def _(step):
        rows = pl.ds(pl.multiple_of(step * length, length), length)
        plane_high[rows, :], plane_low[rows, :] = split_field(outer[pl.ds(step, 1), :] * inner[...])

    for p in range(share):
        moved = shift(boxes[share + p].astype(F32), moves[p, 0], moves[p, 1], moves[p, 2])
        shifts[p] = moved
        fields[p * length : (p + 1) * length, :] = boxes[p].astype(F32) * moved
    along_plane()
    for p in range(share):
        rows = slice(p * length, (p + 1) * length)
        fields[rows, :] = along_x(along_x(fields[rows, :]) * green[...])
    along_plane()
    for p in range(share):
        potential = fields[p * length : (p + 1) * length, :]
        out[p] = potential * shifts[p]
        out[share + p] = shift(
            potential * boxes[p].astype(F32), -moves[p, 0], -moves[p, 1], -moves[p, 2]
        )


def whole_terms(boxes, moves):
    count, length, cells = boxes.shape
    share = count // 2
    vmem = pl.BlockSpec(memory_space=pltpu.VMEM)
    return pl.pallas_call(
        pair_kernel,
        out_shape=jax.ShapeDtypeStruct((count, length, cells), F32),
        in_specs=[pl.BlockSpec(memory_space=pltpu.SMEM)] + [vmem] * 6,
        out_specs=vmem,
        scratch_shapes=[
            pltpu.VMEM((share, length, cells), F32),
            pltpu.VMEM((share * length, cells), F32),
            pltpu.VMEM((cells, cells), BF16),
            pltpu.VMEM((cells, cells), BF16),
        ],
        compiler_params=pltpu.CompilerParams(vmem_limit_bytes=48 * 1024 * 1024),
    )(moves, boxes, *[jnp.asarray(t) for t in fixed_tables(length)])


def per_device(orbitals, pair_list, offsets):
    groups = lax.axis_size("orb")
    layers = lax.axis_size("grp")
    owner_index = lax.axis_index("orb")
    region = lax.axis_index("grp")
    slab_depth = orbitals.shape[1]
    plane_cells = orbitals.shape[2]
    slot_count = groups * CAP
    cell_count = slab_depth * plane_cells
    own_pairs = lax.dynamic_index_in_dim(pair_list, owner_index, 0, keepdims=False)
    slot_ids = jnp.arange(slot_count, dtype=jnp.int32)
    send_match = own_pairs[None, :, 2] == slot_ids[:, None]
    send_valid = jnp.any(send_match, axis=1)
    source = jnp.sum(jnp.where(send_match, own_pairs[None, :, 0], 0), axis=1)
    outgoing = jnp.take(orbitals, source, axis=0) * send_valid[:, None, None].astype(jnp.bfloat16)
    incoming = lax.all_to_all(outgoing, "orb", split_axis=0, concat_axis=0, tiled=True)
    wanted = owner_index * CAP + jnp.arange(CAP, dtype=jnp.int32)
    recv_match = pair_list[:, None, :, 2] == wanted[None, :, None]
    recv_valid = jnp.any(recv_match, axis=2).reshape(slot_count)
    first_local = jnp.sum(jnp.where(recv_match, pair_list[:, None, :, 1], 0), axis=2).reshape(
        slot_count
    )
    second_local = jnp.sum(jnp.where(recv_match, pair_list[:, None, :, 0], 0), axis=2)
    second_ids = (jnp.arange(groups, dtype=jnp.int32)[:, None] * ORB_GRP + second_local).reshape(
        slot_count
    )
    first_ids = owner_index * ORB_GRP + first_local
    displace = jnp.take(offsets, second_ids, axis=0) - jnp.take(offsets, first_ids, axis=0)
    first_box = jnp.take(orbitals, first_local, axis=0)
    share_count = slot_count // layers
    by_region = (layers, share_count, slab_depth, plane_cells)
    both = jnp.concatenate([first_box.reshape(by_region), incoming.reshape(by_region)], axis=1)
    both = both.reshape(2 * slot_count, slab_depth, plane_cells)
    both_whole = lax.all_to_all(both, "grp", split_axis=0, concat_axis=1, tiled=True)
    part_moves = lax.dynamic_slice_in_dim(displace, region * share_count, share_count, 0)
    terms = whole_terms(both_whole, part_moves)
    terms = lax.all_to_all(terms, "grp", split_axis=1, concat_axis=0, tiled=True)
    terms = terms.reshape(layers, 2, share_count, slab_depth, plane_cells)
    to_first_slab = terms[:, 0].reshape(slot_count, slab_depth, plane_cells)
    returned_slab = terms[:, 1].reshape(slot_count, slab_depth, plane_cells)
    returned_home = lax.all_to_all(returned_slab, "orb", split_axis=0, concat_axis=0, tiled=True)
    local_ids = jnp.arange(orbitals.shape[0], dtype=jnp.int32)
    send_hot = (source[None, :] == local_ids[:, None]) & send_valid[None, :]
    recv_hot = (first_local[None, :] == local_ids[:, None]) & recv_valid[None, :]
    hot = jnp.concatenate([send_hot, recv_hot], axis=1).astype(BF16)
    landed = jnp.concatenate([returned_home, to_first_slab], axis=0)
    landed = landed.reshape(2 * slot_count, cell_count)
    high = lax.reduce_precision(landed, 8, 7)
    rest = landed - high
    action = dot(hot, high.astype(BF16)) + dot(hot, rest.astype(BF16))
    return action.reshape(orbitals.shape)


def solution(mesh):
    in_specs = (P("orb", "grp", None), P(), P())
    out_specs = P("orb", "grp", None)
    return jax.shard_map(
        per_device, mesh=mesh, in_specs=in_specs, out_specs=out_specs, check_vma=False
    )
```

profile of v0, /device:TPU:0, one launch (start us, length us, event | category | flops | bytes accessed | tf_op | source)
XLA Modules:
  0.0 77.5 jit_solution(5526314253550851636)
XLA Ops:
  0.0 0.8 %slice_bitcast_fusion.1 = (s32[8,8]{1,0:T(8,128)S(1)}, s32[8,8]{1,0:T(8,128)S(1)}, s32[8,8]{1,0:T(8,128)S(1)}) fusion(s32[8,8,3]{1,0,2:T(8,128)} %param.13), kind=kLoop, calls=%fused_computation.30 | loop fusion | bytes 1536 | tf_op jit(solution)/shard_map/jit(_where)/broadcast_in_dim | solution.py:144
  0.8 0.7 constant_dynamic-slice_fusion
  2.2 0.6 gather_fusion.3
  2.7 0.8 %select_multiply_fusion = bf16[16,8,1024]{2,1,0:T(8,128)(2,1)} fusion(bf16[16,8,1024]{2,1,0:T(8,128)(2,1)S(1)} %gather_fusion.3, pred[16]{0:T(512)(128)(4,1)S(1)} %get-tuple-element.21, bf16[16]{0:T(256)(128)(2,1)S(1)} %convert_element_type.15), kind=kLoop, calls=%fused_computation.11 | loop fusion | flops 262144 | bytes 524336 | tf_op jit(solution)/shard_map/mul | solution.py:139
  3.5 6.4 %all-to-all-start = ((bf16[16,8,1024]{2,1,0:T(8,128)(2,1)}), bf16[16,8,1024]{2,1,0:T(8,128)(2,1)S(1)}, u32[]{:S(2)}, u32[]{:S(2)}) async-start(bf16[16,8,1024]{2,1,0:T(8,128)(2,1)} %select_multiply_fusion), calls=%async_computation | async-start | bytes 524288 | tf_op jit(solution)/shard_map/all_to_all | solution.py:140
  10.3 0.6 gather_fusion.2
  11.2 8.4 %all-to-all-done = bf16[16,8,1024]{2,1,0:T(8,128)(2,1)S(1)} async-done(((bf16[16,8,1024]{2,1,0:T(8,128)(2,1)}), bf16[16,8,1024]{2,1,0:T(8,128)(2,1)S(1)}, u32[]{:S(2)}, u32[]{:S(2)}) %all-to-all-start) | async-done | bytes 262176 | tf_op jit(solution)/shard_map/all_to_all | solution.py:140
  19.6 0.8 %pad_maximum_fusion = bf16[4,8,8,1024]{3,2,1,0:T(8,128)(2,1)} fusion(bf16[4,4,8,1024]{3,2,1,0:T(8,128)(2,1)S(1)} %bitcast.44, bf16[4,4,8,1024]{3,2,1,0:T(8,128)(2,1)S(1)} %bitcast.43), kind=kLoop, calls=%fused_computation.9 | loop fusion | flops 262144 | bytes 1048576 | tf_op jit(solution)/shard_map/concatenate | solution.py:156
  20.4 3.7 %all-to-all-start.1 = ((bf16[32,8,1024]{2,1,0:T(8,128)(2,1)}), bf16[32,8,1024]{2,1,0:T(8,128)(2,1)S(1)}, u32[]{:S(2)}, u32[]{:S(2)}) async-start(bf16[32,8,1024]{2,1,0:T(8,128)(2,1)} %bitcast.7), calls=%async_computation.1 | async-start | bytes 1048576 | tf_op jit(solution)/shard_map/all_to_all | solution.py:158
  24.2 0.6 gather_fusion.1
  24.8 0.6 gather_fusion
  25.4 6.4 %all-to-all-done.1 = bf16[32,8,1024]{2,1,0:T(8,128)(2,1)S(1)} async-done(((bf16[32,8,1024]{2,1,0:T(8,128)(2,1)}), bf16[32,8,1024]{2,1,0:T(8,128)(2,1)S(1)}, u32[]{:S(2)}, u32[]{:S(2)}) %all-to-all-start.1) | async-done | bytes 524320 | tf_op jit(solution)/shard_map/all_to_all | solution.py:158
  31.9 5.1 %shard_map.82 = f32[8,32,1024]{2,1,0:T(8,128)S(1)} custom-call(s32[4,3]{1,0:T(4,128)S(1)} %fusion.8.moves, bf16[8,32,1024]{2,1,0:T(8,128)(2,1)S(1)} %bitcast.34, f32[32,1024]{1,0:T(8,128)S(1)} %copy-done.3, f32[32,1024]{1,0:T(8,128)S(1)} %copy-done.2, bf16[32,32]{1,0:T(8,128)(2,1)S(1)} %copy-done.5, bf16[32,32]{1,0:T(8,128)(2,1)S(1)} %copy-done.4, ...), custom_call_target="tpu_custom_call" | custom-call | tf_op jit(solution)/shard_map/pallas_call | solution.py:110
  37.0 0.6 copy.34
  37.6 15.4 %all_to_all.43 = f32[8,32,1024]{2,0,1:T(8,128)S(1)} all-to-all(f32[8,32,1024]{2,0,1:T(8,128)S(1)} %copy.34), channel_id=1, replica_groups=mesh['orb'=8,'grp'=4] {'grp'}, dimensions={1} | all-to-all | bytes 2097152 | tf_op jit(solution)/shard_map/all_to_all | solution.py:161
  53.0 0.6 copy.36
  53.6 0.9 %fusion.9 = (f32[4,1,4,8,1024]{4,3,2,1,0:T(8,128)S(1)}, f32[4,1,4,8,1024]{4,3,2,1,0:T(8,128)}) fusion(f32[4,2,4,8,1024]{4,3,2,1,0:T(8,128)S(1)} %bitcast.36), kind=kLoop, calls=%fused_computation.53 | loop fusion | bytes 2097152 | tf_op jit(solution)/shard_map/slice | solution.py:163
  54.5 3.7 %all-to-all-start.3 = ((f32[16,8,1024]{2,1,0:T(8,128)}), f32[16,8,1024]{2,1,0:T(8,128)S(1)}, u32[]{:S(2)}, u32[]{:S(2)}) async-start(f32[16,8,1024]{2,1,0:T(8,128)} %bitcast.15), calls=%async_computation.3 | async-start | bytes 1048576 | tf_op jit(solution)/shard_map/all_to_all | solution.py:165
  58.7 0.3 copy.40
  59.0 14.6 %all-to-all-done.3 = f32[16,8,1024]{2,1,0:T(8,128)S(1)} async-done(((f32[16,8,1024]{2,1,0:T(8,128)}), f32[16,8,1024]{2,1,0:T(8,128)S(1)}, u32[]{:S(2)}, u32[]{:S(2)}) %all-to-all-start.3) | async-done | bytes 524320 | tf_op jit(solution)/shard_map/all_to_all | solution.py:165
  73.6 0.3 copy.39
  74.0 0.5 fusion.2
  74.5 0.5 convolution_add_fusion
  75.0 2.5 %copy.41 = f32[8,8,8,1024]{3,2,1,0:T(8,128)} copy(f32[8,8,8,1024]{3,1,2,0:T(8,128)S(1)} %bitcast.35) | data formatting | bytes 4194304
  (48 shorter events, 1.8 us)
Async XLA Ops:
  0.0 2.2 %copy-start = (bf16[64,8,1024]{2,1,0:T(8,128)(2,1)S(1)}, bf16[64,8,1024]{2,1,0:T(8,128)(2,1)}, u32[]{:S(2)}) copy-start(bf16[64,8,1024]{2,1,0:T(8,128)(2,1)} %param.12) | copy-start | bytes 3145732
  0.0 10.8 %copy-start.6 = (s32[512,3]{0,1:T(4,128)S(1)}, s32[512,3]{0,1:T(4,128)}, u32[]{:S(2)}) copy-start(s32[512,3]{0,1:T(4,128)} %param.14) | copy-start | bytes 18436
  3.5 16.1 %all-to-all-start = ((bf16[16,8,1024]{2,1,0:T(8,128)(2,1)}), bf16[16,8,1024]{2,1,0:T(8,128)(2,1)S(1)}, u32[]{:S(2)}, u32[]{:S(2)}) async-start(bf16[16,8,1024]{2,1,0:T(8,128)(2,1)} %select_multiply_fusion), calls=%async_computation | async-start | bytes 524288 | tf_op jit(solution)/shard_map/all_to_all | solution.py:140
  10.8 21.0 %copy-start.1 = (f32[32,1024]{1,0:T(8,128)S(1)}, f32[32,1024]{1,0:T(8,128)}, u32[]{:S(2)}) copy-start(f32[32,1024]{1,0:T(8,128)} %constant.61.clone.green) | copy-start | bytes 393220
  10.9 21.0 %copy-start.2 = (f32[32,1024]{1,0:T(8,128)S(1)}, f32[32,1024]{1,0:T(8,128)}, u32[]{:S(2)}) copy-start(f32[32,1024]{1,0:T(8,128)} %constant.58.clone.inner) | copy-start | bytes 393220
  10.9 21.0 %copy-start.3 = (f32[32,1024]{1,0:T(8,128)S(1)}, f32[32,1024]{1,0:T(8,128)}, u32[]{:S(2)}) copy-start(f32[32,1024]{1,0:T(8,128)} %constant.24.clone.outer) | copy-start | bytes 393220
  10.9 21.0 %copy-start.4 = (bf16[32,32]{1,0:T(8,128)(2,1)S(1)}, bf16[32,32]{1,0:T(8,128)(2,1)}, u32[]{:S(2)}) copy-start(bf16[32,32]{1,0:T(8,128)(2,1)} %constant.60.clone.sine_low) | copy-start | bytes 6148
  10.9 21.0 %copy-start.5 = (bf16[32,32]{1,0:T(8,128)(2,1)S(1)}, bf16[32,32]{1,0:T(8,128)(2,1)}, u32[]{:S(2)}) copy-start(bf16[32,32]{1,0:T(8,128)(2,1)} %constant.59.clone.sine_high) | copy-start | bytes 6148
  20.4 11.4 %all-to-all-start.1 = ((bf16[32,8,1024]{2,1,0:T(8,128)(2,1)}), bf16[32,8,1024]{2,1,0:T(8,128)(2,1)S(1)}, u32[]{:S(2)}, u32[]{:S(2)}) async-start(bf16[32,8,1024]{2,1,0:T(8,128)(2,1)} %bitcast.7), calls=%async_computation.1 | async-start | bytes 1048576 | tf_op jit(solution)/shard_map/all_to_all | solution.py:158
  54.5 19.1 %all-to-all-start.3 = ((f32[16,8,1024]{2,1,0:T(8,128)}), f32[16,8,1024]{2,1,0:T(8,128)S(1)}, u32[]{:S(2)}, u32[]{:S(2)}) async-start(f32[16,8,1024]{2,1,0:T(8,128)} %bitcast.15), calls=%async_computation.3 | async-start | bytes 1048576 | tf_op jit(solution)/shard_map/all_to_all | solution.py:165
where the time goes:
time: 77.9 us; the launch traced here: 77.5 us
  waiting for transfers between devices  29.4 us (38%)
  blocking collectives  15.4 us (20%)
  starting transfers between devices  13.8 us (18%)
  local copies, waits for them, and re-layouts  9.99 us (13%)
  Pallas kernels  5.07 us (7%)
  other arithmetic  2.52 us (3%)
  matrix products  0.96 us (1%)
    all_to_all x1, blocking collectives, per_device(): lax.all_to_all(terms, 'grp', split_axis=1, concat_axis=0, tiled=True)  15.4 us
    all_to_all x1, waiting for transfers between devices, per_device(): lax.all_to_all(returned_slab, 'orb', split_axis=0, concat_axis=0, tiled=T...  14.6 us
    all_to_all x1, waiting for transfers between devices, per_device(): lax.all_to_all(outgoing, 'orb', split_axis=0, concat_axis=0, tiled=True)  8.44 us
    all_to_all x1, waiting for transfers between devices, per_device(): lax.all_to_all(both, 'grp', split_axis=0, concat_axis=1, tiled=True)  6.43 us
    all_to_all x1, starting transfers between devices, per_device(): lax.all_to_all(outgoing, 'orb', split_axis=0, concat_axis=0, tiled=True)  6.36 us
    pallas_call x1, Pallas kernels, whole_terms(): pl.pallas_call(pair_kernel, out_shape=jax.ShapeDtypeStruct((count, length...  5.07 us
    all_to_all x1, starting transfers between devices, per_device(): lax.all_to_all(returned_slab, 'orb', split_axis=0, concat_axis=0, tiled=T...  3.74 us
    all_to_all x1, starting transfers between devices, per_device(): lax.all_to_all(both, 'grp', split_axis=0, concat_axis=1, tiled=True)  3.72 us
  transfers between devices with their start and end apart: 3, of which 3 were waited for; matrix products, arithmetic and copies ran while one was open for 4% of the time, Pallas kernels for 0%

commit v1 on v0

v1 whole, which is shorter than its diff:
```python
import math

import jax
import jax.numpy as jnp
import ml_dtypes
import numpy as np
from jax import lax
from jax.experimental import pallas as pl
from jax.experimental.pallas import tpu as pltpu
from jax.sharding import PartitionSpec as P

MESH = pl.DeviceIdType.MESH
SHIFT = 0.25
F32 = jnp.float32
BF16 = jnp.bfloat16


def split_table(table):
    wide = np.asarray(table, np.float32)
    high = wide.astype(ml_dtypes.bfloat16)
    low = (wide - high.astype(np.float32)).astype(ml_dtypes.bfloat16)
    return high, low


def fixed_tables(length):
    counts = np.arange(length) + 1.0
    sine = np.sqrt(2.0 / (length + 1.0)) * np.sin(
        math.pi * counts[:, None] * counts[None, :] / (length + 1.0)
    )
    levels = 2.0 - 2.0 * np.cos(math.pi * counts / (length + 1.0))
    green = 1.0 / (
        levels[:, None, None] + levels[None, :, None] + levels[None, None, :] + SHIFT
    )
    ones = np.ones((1, length))
    return (
        np.kron(sine, ones).astype(np.float32),
        np.kron(ones, sine).astype(np.float32),
        *split_table(sine),
        green.reshape(length, length * length).astype(np.float32),
    )


def split_field(field):
    high = field.astype(BF16)
    return high, (field - high.astype(F32)).astype(BF16)


def dot(left, right):
    return jnp.dot(left, right, preferred_element_type=F32)


def ring_order(count):
    return sorted(range(1, count), key=lambda k: -min(k, count - k))


def find(pairs, block, wanted, what, rows):
    value = jnp.int32(0)
    valid = jnp.int32(0)
    for r in range(rows):
        hit = pairs[2, block, r] == wanted
        value = jnp.where(hit, jnp.int32(r) if what is None else pairs[what, block, r], value)
        valid = jnp.where(hit, jnp.int32(1), valid)
    return value, valid


def exchange_kernel(
    pairs, offsets, orbitals, outer, inner, sine_high, sine_low, green,
    landed, home,
    send_a, recv_a, stage_i, stage_j, box_i, box_j, field, shifted, second, plane_high, plane_low,
    term_i, term_j, rows_i, send_d, recv_d, rows_j,
    sem_sa, sem_ra, sem_si, sem_ri, sem_sj, sem_rj, sem_st, sem_rt, sem_su, sem_ru, sem_sd, sem_rd,
):
    groups, cap, depth, cells = send_a.shape
    regions, share = box_i.shape[:2]
    rows = regions * share
    length = regions * depth
    local_count = orbitals.shape[0]
    me = lax.axis_index("orb")
    region = lax.axis_index("grp")
    orb_steps = ring_order(groups)
    grp_steps = ring_order(regions)

    def orb_peer(k):
        return lax.rem(me + k, groups)

    def grp_peer(k):
        return lax.rem(region + k, regions)

    barrier = pltpu.get_barrier_semaphore()
    for k in orb_steps:
        pl.semaphore_signal(barrier, inc=1, device_id={"orb": orb_peer(k)}, device_id_type=MESH)
    for k in grp_steps:
        pl.semaphore_signal(barrier, inc=1, device_id={"grp": grp_peer(k)}, device_id_type=MESH)

    for block in range(groups):
        for c in range(cap):
            local, _ = find(pairs, block, me * cap + c, 1, rows)
            send_a[block, c] = orbitals[local]
    for r in range(rows):
        stage_j[r] = orbitals[pairs[0, me, r]]
    pl.semaphore_wait(barrier, groups + regions - 2)

    copies_a = []
    for k in orb_steps:
        peer = orb_peer(k)
        copy = pltpu.make_async_remote_copy(
            src_ref=send_a.at[peer], dst_ref=recv_a.at[me],
            send_sem=sem_sa.at[peer], recv_sem=sem_ra.at[me],
            device_id={"orb": peer}, device_id_type=MESH)
        copy.start()
        copies_a.append(copy)

    def grp_send(source, target, send_sem, recv_sem):
        copies = []
        for k in grp_steps:
            peer = grp_peer(k)
            copy = pltpu.make_async_remote_copy(
                src_ref=source(peer), dst_ref=target(region),
                send_sem=send_sem.at[peer], recv_sem=recv_sem.at[region],
                device_id={"grp": peer}, device_id_type=MESH)
            copy.start()
            copies.append(copy)
        return copies

    def grp_wait(source, target, send_sem, recv_sem):
        for k in grp_steps:
            peer = grp_peer(k)
            pltpu.make_async_remote_copy(
                src_ref=source(peer), dst_ref=target(peer),
                send_sem=send_sem.at[peer], recv_sem=recv_sem.at[peer],
                device_id={"grp": peer}, device_id_type=MESH).wait_recv()

    def share_rows(ref):
        return lambda part: ref.at[pl.ds(part * share, share)]

    def whole(ref):
        return lambda part: ref.at[part]

    j_args = (share_rows(stage_j), whole(box_j), sem_sj, sem_rj)
    i_args = (share_rows(stage_i), whole(box_i), sem_si, sem_ri)
    t_args = (whole(term_i), share_rows(rows_i), sem_st, sem_rt)
    u_args = (whole(term_j), share_rows(rows_j), sem_su, sem_ru)

    copies = grp_send(*j_args)
    for c in range(cap):
        recv_a[me, c] = send_a[me, c]
    for p in range(share):
        box_j[region, p] = stage_j[region * share + p]

    @pl.loop(0, length)
    def _(step):
        span = pl.ds(pl.multiple_of(step * length, length), length)
        plane_high[span, :], plane_low[span, :] = split_field(outer[pl.ds(step, 1), :] * inner[...])

    row = lax.broadcasted_iota(jnp.int32, (length, cells), 0)
    col = lax.broadcasted_iota(jnp.int32, (length, cells), 1)
    mid = col // length
    last = col - mid * length

    def shift(values, dx, dy, dz):
        moved = pltpu.roll(values, jnp.remainder(-dx + length, length), 0)
        flat = jnp.remainder(2 * cells - dy * length - dz, cells)
        moved = pltpu.roll(moved, flat, 1)
        x, y, z = row + dx, mid + dy, last + dz
        keep = (x >= 0) & (x < length) & (y >= 0) & (y < length) & (z >= 0) & (z < length)
        return jnp.where(keep, moved, 0.0)

    moves = []
    for p in range(share):
        r = region * share + p
        j = me * local_count + pairs[0, me, r]
        i = (pairs[2, me, r] // cap) * local_count + pairs[1, me, r]
        moves.append([offsets[a, j] - offsets[a, i] for a in range(3)])

    grp_wait(*j_args)
    for p in range(share):
        for part in range(regions):
            field[part * depth : (part + 1) * depth, :] = box_j[part, p].astype(F32)
        shifted[p] = shift(field[0:length, :], *moves[p])

    for k in orb_steps:
        peer = orb_peer(k)
        pltpu.make_async_remote_copy(
            src_ref=send_a.at[peer], dst_ref=recv_a.at[peer],
            send_sem=sem_sa.at[peer], recv_sem=sem_ra.at[peer],
            device_id={"orb": peer}, device_id_type=MESH).wait_recv()
    for r in range(rows):
        slot = pairs[2, me, r]
        stage_i[r] = recv_a[slot // cap, slot % cap]
    copies += grp_send(*i_args)
    for p in range(share):
        box_i[region, p] = stage_i[region * share + p]
    grp_wait(*i_args)

    for p in range(share):
        for part in range(regions):
            span = slice(part * depth, (part + 1) * depth)
            second[p, span, :] = box_i[part, p].astype(F32)
        field[p * length : (p + 1) * length, :] = second[p] * shifted[p]

    def along_plane():
        high, low = split_field(field[...])
        field[...] = (
            dot(high, plane_high[...]) + dot(low, plane_high[...]) + dot(high, plane_low[...])
        )

    def along_x(values):
        high, low = split_field(values)
        return dot(sine_high[...], high) + dot(sine_high[...], low) + dot(sine_low[...], high)

    along_plane()
    for p in range(share):
        span = slice(p * length, (p + 1) * length)
        field[span, :] = along_x(along_x(field[span, :]) * green[...])
    along_plane()
    for p in range(share):
        term = field[p * length : (p + 1) * length, :] * shifted[p]
        for part in range(regions):
            term_i[part, p] = term[part * depth : (part + 1) * depth, :]
    copies += grp_send(*t_args)
    for p in range(share):
        rows_i[region * share + p] = term_i[region, p]
        term = shift(field[p * length : (p + 1) * length, :] * second[p], *[-d for d in moves[p]])
        for part in range(regions):
            term_j[part, p] = term[part * depth : (part + 1) * depth, :]
    copies += grp_send(*u_args)
    for p in range(share):
        rows_j[region * share + p] = term_j[region, p]

    grp_wait(*t_args)
    for k in orb_steps + [0]:
        peer = orb_peer(k)
        for c in range(cap):
            r, _ = find(pairs, me, peer * cap + c, None, rows)
            send_d[peer, c] = rows_i[r]
        if k == 0:
            break
        copy = pltpu.make_async_remote_copy(
            src_ref=send_d.at[peer], dst_ref=recv_d.at[me],
            send_sem=sem_sd.at[peer], recv_sem=sem_rd.at[me],
            device_id={"orb": peer}, device_id_type=MESH)
        copy.start()
        copies_a.append(copy)
    for c in range(cap):
        recv_d[me, c] = send_d[me, c]
    grp_wait(*u_args)
    home[...] = rows_j[...]
    for k in orb_steps:
        peer = orb_peer(k)
        pltpu.make_async_remote_copy(
            src_ref=send_d.at[peer], dst_ref=recv_d.at[peer],
            send_sem=sem_sd.at[peer], recv_sem=sem_rd.at[peer],
            device_id={"orb": peer}, device_id_type=MESH).wait_recv()
    landed[...] = recv_d[...]
    for copy in copies_a + copies:
        copy.wait_send()


def exchange_terms(pairs, offsets, orbitals, groups, regions):
    _, depth, cells = orbitals.shape
    rows = pairs.shape[2]
    share = rows // regions
    cap = 2 * rows // groups
    length = depth * regions
    vmem = pl.BlockSpec(memory_space=pltpu.VMEM)
    smem = pl.BlockSpec(memory_space=pltpu.SMEM)
    by_slot = (groups, cap, depth, cells)
    by_row = (rows, depth, cells)
    by_region = (regions, share, depth, cells)
    dma = pltpu.SemaphoreType.DMA
    return pl.pallas_call(
        exchange_kernel,
        out_shape=(jax.ShapeDtypeStruct(by_slot, F32), jax.ShapeDtypeStruct(by_row, F32)),
        in_specs=[smem, smem] + [vmem] * 6,
        out_specs=(vmem, vmem),
        scratch_shapes=[
            pltpu.VMEM(by_slot, BF16), pltpu.VMEM(by_slot, BF16),
            pltpu.VMEM(by_row, BF16), pltpu.VMEM(by_row, BF16),
            pltpu.VMEM(by_region, BF16), pltpu.VMEM(by_region, BF16),
            pltpu.VMEM((share * length, cells), F32),
            pltpu.VMEM((share, length, cells), F32),
            pltpu.VMEM((share, length, cells), F32),
            pltpu.VMEM((cells, cells), BF16), pltpu.VMEM((cells, cells), BF16),
            pltpu.VMEM(by_region, F32), pltpu.VMEM(by_region, F32),
            pltpu.VMEM(by_row, F32),
            pltpu.VMEM(by_slot, F32), pltpu.VMEM(by_slot, F32),
            pltpu.VMEM(by_row, F32),
            dma((groups,)), dma((groups,)),
            dma((regions,)), dma((regions,)), dma((regions,)), dma((regions,)),
            dma((regions,)), dma((regions,)), dma((regions,)), dma((regions,)),
            dma((groups,)), dma((groups,)),
        ],
        compiler_params=pltpu.CompilerParams(
            collective_id=0, has_side_effects=True, vmem_limit_bytes=32 * 1024 * 1024),
    )(pairs, offsets, orbitals, *[jnp.asarray(t) for t in fixed_tables(length)])


def collect_kernel(pairs, landed, home, out):
    groups, cap = landed.shape[:2]
    rows = home.shape[0]
    me = lax.axis_index("orb")
    out[...] = jnp.zeros_like(out)
    for r in range(rows):
        k = pairs[0, me, r]
        out[k] += home[r]
    for block in range(groups):
        for c in range(cap):
            k, valid = find(pairs, block, me * cap + c, 1, rows)
            out[k] += jnp.where(valid > 0, landed[block, c], 0.0)


def collect(pairs, landed, home, shape):
    vmem = pl.BlockSpec(memory_space=pltpu.VMEM)
    smem = pl.BlockSpec(memory_space=pltpu.SMEM)
    return pl.pallas_call(
        collect_kernel,
        out_shape=jax.ShapeDtypeStruct(shape, F32),
        in_specs=[smem, vmem, vmem],
        out_specs=vmem,
        compiler_params=pltpu.CompilerParams(vmem_limit_bytes=32 * 1024 * 1024),
    )(pairs, landed, home)


def per_device(orbitals, pair_list, offsets):
    groups = lax.axis_size("orb")
    regions = lax.axis_size("grp")
    pairs = jnp.transpose(pair_list, (2, 0, 1))
    landed, home = exchange_terms(pairs, offsets.T, orbitals, groups, regions)
    return collect(pairs, landed, home, orbitals.shape)


def solution(mesh):
    in_specs = (P("orb", "grp", None), P(), P())
    out_specs = P("orb", "grp", None)
    return jax.shard_map(
        per_device, mesh=mesh, in_specs=in_specs, out_specs=out_specs, check_vma=False
    )
```

time: 77.9 us -> 44.4 us (0.57)
  the two profiles are of different devices: /device:TPU:0 before, /device:TPU:16 now
where the time goes in v1:
time: 44.4 us; the launch traced here: 44 us
  Pallas kernels  37.3 us (84%)
  local copies, waits for them, and re-layouts  6.73 us (15%)
    pallas_call x1, Pallas kernels, exchange_terms(): pl.pallas_call(exchange_kernel, out_shape=(jax.ShapeDtypeStruct(by_slot,...  34.9 us
    unnamed x16, local copies, waits for them, and re-layouts  6.73 us
    pallas_call x1, Pallas kernels, collect(): pl.pallas_call(collect_kernel, out_shape=jax.ShapeDtypeStruct(shape, F32)...  2.39 us

profile of v1, /device:TPU:16, one launch (start us, length us, event | category | flops | bytes accessed | tf_op | source)
XLA Modules:
  0.0 44.0 jit_solution(13172689301563111373)
XLA Ops:
  0.0 0.0 copy-start
  0.0 1.2 %copy-done = bf16[64,8,1024]{2,1,0:T(8,128)(2,1)S(1)} copy-done((bf16[64,8,1024]{2,1,0:T(8,128)(2,1)S(1)}, bf16[64,8,1024]{2,1,0:T(8,128)(2,1)}, u32[]{:S(2)}) %copy-start) | copy-done | bytes 1048600
  1.2 0.0 copy-start.1
  1.2 0.9 %copy-done.1 = f32[32,1024]{1,0:T(8,128)S(1)} copy-done((f32[32,1024]{1,0:T(8,128)S(1)}, f32[32,1024]{1,0:T(8,128)}, u32[]{:S(2)}) %copy-start.1) | copy-done | bytes 131096
  2.1 0.0 copy-start.2
  2.1 0.9 %copy-done.2 = f32[32,1024]{1,0:T(8,128)S(1)} copy-done((f32[32,1024]{1,0:T(8,128)S(1)}, f32[32,1024]{1,0:T(8,128)}, u32[]{:S(2)}) %copy-start.2) | copy-done | bytes 131096
  3.0 0.0 copy-start.3
  3.0 0.9 %copy-done.3 = f32[32,1024]{1,0:T(8,128)S(1)} copy-done((f32[32,1024]{1,0:T(8,128)S(1)}, f32[32,1024]{1,0:T(8,128)}, u32[]{:S(2)}) %copy-start.3) | copy-done | bytes 131096
  3.9 0.0 copy-start.4
  3.9 0.7 %copy-done.4 = s32[8,8,3]{1,0,2:T(8,128)S(1)} copy-done((s32[8,8,3]{1,0,2:T(8,128)S(1)}, s32[8,8,3]{1,0,2:T(8,128)}, u32[]{:S(2)}) %copy-start.4) | copy-done | bytes 792
  4.6 0.0 copy-start.5
  4.6 0.7 %copy-done.5 = s32[512,3]{0,1:T(4,128)S(1)} copy-done((s32[512,3]{0,1:T(4,128)S(1)}, s32[512,3]{0,1:T(4,128)}, u32[]{:S(2)}) %copy-start.5) | copy-done | bytes 6168
  5.3 0.0 copy-start.6
  5.3 0.7 %copy-done.6 = bf16[32,32]{1,0:T(8,128)(2,1)S(1)} copy-done((bf16[32,32]{1,0:T(8,128)(2,1)S(1)}, bf16[32,32]{1,0:T(8,128)(2,1)}, u32[]{:S(2)}) %copy-start.6) | copy-done | bytes 2072
  6.0 0.0 copy-start.7
  6.0 0.7 %copy-done.7 = bf16[32,32]{1,0:T(8,128)(2,1)S(1)} copy-done((bf16[32,32]{1,0:T(8,128)(2,1)S(1)}, bf16[32,32]{1,0:T(8,128)(2,1)}, u32[]{:S(2)}) %copy-start.7) | copy-done | bytes 2072
  6.7 34.9 %shard_map.82 = (f32[8,2,8,1024]{3,2,1,0:T(8,128)S(1)}, f32[8,8,1024]{2,1,0:T(8,128)S(1)}) custom-call(s32[3,8,8]{2,1,0:T(8,128)S(1)} %bitcast.2, s32[3,512]{1,0:T(4,128)S(1)} %bitcast.4, bf16[64,8,1024]{2,1,0:T(8,128)(2,1)S(1)} %copy-done, f32[32,1024]{1,0:T(8,128)S(1)} %copy-done.3, f32[32,1024]{1,0:T(8,128)S(1)} %copy-done.2, ...), custom_call_target="tpu_custom_call" | custom-call | tf_op jit(solution)/shard_map/pallas_call | solution.py:271
  41.6 2.4 %shard_map.83 = f32[64,8,1024]{2,1,0:T(8,128)} custom-call(s32[3,8,8]{2,1,0:T(8,128)S(1)} %bitcast.3, f32[8,2,8,1024]{3,2,1,0:T(8,128)S(1)} %get-tuple-element.7.landed, f32[8,8,1024]{2,1,0:T(8,128)S(1)} %get-tuple-element.8.home), custom_call_target="tpu_custom_call" | custom-call | tf_op jit(solution)/shard_map/pallas_call | solution.py:315
Async XLA Ops:
  0.0 1.2 %copy-start = (bf16[64,8,1024]{2,1,0:T(8,128)(2,1)S(1)}, bf16[64,8,1024]{2,1,0:T(8,128)(2,1)}, u32[]{:S(2)}) copy-start(bf16[64,8,1024]{2,1,0:T(8,128)(2,1)} %orbitals.1) | copy-start | bytes 3145732
  1.2 0.9 %copy-start.1 = (f32[32,1024]{1,0:T(8,128)S(1)}, f32[32,1024]{1,0:T(8,128)}, u32[]{:S(2)}) copy-start(f32[32,1024]{1,0:T(8,128)} %constant.14.clone.green) | copy-start | bytes 393220
  2.1 0.9 %copy-start.2 = (f32[32,1024]{1,0:T(8,128)S(1)}, f32[32,1024]{1,0:T(8,128)}, u32[]{:S(2)}) copy-start(f32[32,1024]{1,0:T(8,128)} %constant.11.clone.inner) | copy-start | bytes 393220
  3.0 0.9 %copy-start.3 = (f32[32,1024]{1,0:T(8,128)S(1)}, f32[32,1024]{1,0:T(8,128)}, u32[]{:S(2)}) copy-start(f32[32,1024]{1,0:T(8,128)} %constant.10.clone.outer) | copy-start | bytes 393220
  3.9 0.7 %copy-start.4 = (s32[8,8,3]{1,0,2:T(8,128)S(1)}, s32[8,8,3]{1,0,2:T(8,128)}, u32[]{:S(2)}) copy-start(s32[8,8,3]{1,0,2:T(8,128)} %param.9) | copy-start | bytes 2308
  4.6 0.7 %copy-start.5 = (s32[512,3]{0,1:T(4,128)S(1)}, s32[512,3]{0,1:T(4,128)}, u32[]{:S(2)}) copy-start(s32[512,3]{0,1:T(4,128)} %param.10) | copy-start | bytes 18436
  5.3 0.7 %copy-start.6 = (bf16[32,32]{1,0:T(8,128)(2,1)S(1)}, bf16[32,32]{1,0:T(8,128)(2,1)}, u32[]{:S(2)}) copy-start(bf16[32,32]{1,0:T(8,128)(2,1)} %constant.13.clone.sine_low) | copy-start | bytes 6148
  6.0 0.7 %copy-start.7 = (bf16[32,32]{1,0:T(8,128)(2,1)S(1)}, bf16[32,32]{1,0:T(8,128)(2,1)}, u32[]{:S(2)}) copy-start(bf16[32,32]{1,0:T(8,128)(2,1)} %constant.12.clone.sine_high) | copy-start | bytes 6148

commit v2 on v1

--- a/solution.py
+++ b/solution.py
@@ -11,6 +11,7 @@
 
 MESH = pl.DeviceIdType.MESH
 SHIFT = 0.25
+LANES = 128
 F32 = jnp.float32
 BF16 = jnp.bfloat16
 
@@ -63,12 +64,30 @@
     return value, valid
 
 
+LEVELS = 32766.0
+
+
+def encode(values):
+    size = jnp.abs(values)
+    top = jnp.maximum(jnp.max(jnp.max(size, axis=0, keepdims=True), axis=1, keepdims=True), 1e-36)
+    steps = (jnp.sqrt(size * (1.0 / top)) * LEVELS + 0.5).astype(jnp.int32)
+    code = jnp.where(values < 0.0, -steps, steps).astype(jnp.int16)
+    return code, jnp.broadcast_to(top, (1, LANES))
+
+
+def decode(code, top):
+    steps = code.astype(jnp.int32).astype(F32)
+    return steps * jnp.abs(steps) * (top[:, 0:1] * (1.0 / (LEVELS * LEVELS)))
+
+
 def exchange_kernel(
-    pairs, offsets, orbitals, outer, inner, sine_high, sine_low, green,
+    pairs_in, offsets_in, orbitals_in, outer_in, inner_in, sine_high_in, sine_low_in, green_in,
     landed, home,
+    pairs, offsets, orbitals, outer, inner, sine_high, sine_low, green, sem_in,
     send_a, recv_a, stage_i, stage_j, box_i, box_j, field, shifted, second, plane_high, plane_low,
-    term_i, term_j, rows_i, send_d, recv_d, rows_j,
+    term_i, term_j, rows_i, send_d, recv_d, rows_j, top_i, top_rows, send_top, recv_top,
     sem_sa, sem_ra, sem_si, sem_ri, sem_sj, sem_rj, sem_st, sem_rt, sem_su, sem_ru, sem_sd, sem_rd,
+    sem_sv, sem_rv, sem_sw, sem_rw,
 ):
     groups, cap, depth, cells = send_a.shape
     regions, share = box_i.shape[:2]
@@ -86,11 +105,23 @@
     def grp_peer(k):
         return lax.rem(region + k, regions)
 
+    loads = [
+        pltpu.make_async_copy(source, target, sem_in.at[n])
+        for n, (source, target) in enumerate((
+            (pairs_in, pairs), (orbitals_in, orbitals), (offsets_in, offsets),
+            (outer_in, outer), (inner_in, inner), (green_in, green),
+            (sine_high_in, sine_high), (sine_low_in, sine_low)))
+    ]
+    for load in loads:
+        load.start()
     barrier = pltpu.get_barrier_semaphore()
     for k in orb_steps:
         pl.semaphore_signal(barrier, inc=1, device_id={"orb": orb_peer(k)}, device_id_type=MESH)
     for k in grp_steps:
         pl.semaphore_signal(barrier, inc=1, device_id={"grp": grp_peer(k)}, device_id_type=MESH)
+
+    loads[0].wait()
+    loads[1].wait()
 
     for block in range(groups):
         for c in range(cap):
@@ -139,6 +170,7 @@
     j_args = (share_rows(stage_j), whole(box_j), sem_sj, sem_rj)
     i_args = (share_rows(stage_i), whole(box_i), sem_si, sem_ri)
     t_args = (whole(term_i), share_rows(rows_i), sem_st, sem_rt)
+    v_args = (whole(top_i), whole(top_rows), sem_sv, sem_rv)
     u_args = (whole(term_j), share_rows(rows_j), sem_su, sem_ru)
 
     copies = grp_send(*j_args)
@@ -146,6 +178,9 @@
         recv_a[me, c] = send_a[me, c]
     for p in range(share):
         box_j[region, p] = stage_j[region * share + p]
+
+    for load in loads[2:]:
+        load.wait()
 
     @pl.loop(0, length)
     def _(step):
@@ -214,12 +249,16 @@
         field[span, :] = along_x(along_x(field[span, :]) * green[...])
     along_plane()
     for p in range(share):
-        term = field[p * length : (p + 1) * length, :] * shifted[p]
+        code, top = encode(field[p * length : (p + 1) * length, :] * shifted[p])
         for part in range(regions):
-            term_i[part, p] = term[part * depth : (part + 1) * depth, :]
+            term_i[part, p] = code[part * depth : (part + 1) * depth, :]
+            top_i[part, p : p + 1] = top
     copies += grp_send(*t_args)
+    copies += grp_send(*v_args)
     for p in range(share):
         rows_i[region * share + p] = term_i[region, p]
+    top_rows[region] = top_i[region]
+    for p in range(share):
         term = shift(field[p * length : (p + 1) * length, :] * second[p], *[-d for d in moves[p]])
         for part in range(regions):
             term_j[part, p] = term[part * depth : (part + 1) * depth, :]
@@ -228,30 +267,41 @@
         rows_j[region * share + p] = term_j[region, p]
 
     grp_wait(*t_args)
-    for k in orb_steps + [0]:
-        peer = orb_peer(k)
+    grp_wait(*v_args)
+    for peer in range(groups):
         for c in range(cap):
             r, _ = find(pairs, me, peer * cap + c, None, rows)
             send_d[peer, c] = rows_i[r]
-        if k == 0:
-            break
-        copy = pltpu.make_async_remote_copy(
-            src_ref=send_d.at[peer], dst_ref=recv_d.at[me],
-            send_sem=sem_sd.at[peer], recv_sem=sem_rd.at[me],
+            send_top[peer, c : c + 1] = top_rows[r // share, pl.ds(r % share, 1)]
+
+    d_args = (send_d, recv_d, sem_sd, sem_rd)
+    w_args = (send_top, recv_top, sem_sw, sem_rw)
+
+    def orb_copy(k, arriving, source, target, send_sem, recv_sem):
+        peer = orb_peer(k)
+        place = peer if arriving else me
+        return pltpu.make_async_remote_copy(
+            src_ref=source.at[peer], dst_ref=target.at[place],
+            send_sem=send_sem.at[peer], recv_sem=recv_sem.at[place],
             device_id={"orb": peer}, device_id_type=MESH)
-        copy.start()
-        copies_a.append(copy)
-    for c in range(cap):
-        recv_d[me, c] = send_d[me, c]
+
+    for k in orb_steps:
+        for args in (w_args, d_args):
+            copy = orb_copy(k, False, *args)
+            copy.start()
+            copies_a.append(copy)
+
+    def arrived(source, codes, tops):
+        for c in range(cap):
+            landed[source, c] = decode(codes[source, c], tops[source, c : c + 1])
+
+    arrived(me, send_d, send_top)
     grp_wait(*u_args)
     home[...] = rows_j[...]
-    for k in orb_steps:
-        peer = orb_peer(k)
-        pltpu.make_async_remote_copy(
-            src_ref=send_d.at[peer], dst_ref=recv_d.at[peer],
-            send_sem=sem_sd.at[peer], recv_sem=sem_rd.at[peer],
-            device_id={"orb": peer}, device_id_type=MESH).wait_recv()
-    landed[...] = recv_d[...]
+    for k in orb_steps[::-1]:
+        for args in (w_args, d_args):
+            orb_copy(k, True, *args).wait_recv()
+        arrived(orb_peer(k), recv_d, recv_top)
     for copy in copies_a + copies:
         copy.wait_send()
 
@@ -263,7 +313,9 @@
     cap = 2 * rows // groups
     length = depth * regions
     vmem = pl.BlockSpec(memory_space=pltpu.VMEM)
-    smem = pl.BlockSpec(memory_space=pltpu.SMEM)
+    tables = [jnp.asarray(t) for t in fixed_tables(length)]
+    operands = (pairs, offsets, orbitals, *tables)
+    spaces = [pltpu.SMEM, pltpu.SMEM] + [pltpu.VMEM] * 6
     by_slot = (groups, cap, depth, cells)
     by_row = (rows, depth, cells)
     by_region = (regions, share, depth, cells)
@@ -271,9 +323,11 @@
     return pl.pallas_call(
         exchange_kernel,
         out_shape=(jax.ShapeDtypeStruct(by_slot, F32), jax.ShapeDtypeStruct(by_row, F32)),
-        in_specs=[smem, smem] + [vmem] * 6,
+        in_specs=[pl.BlockSpec(memory_space=pltpu.HBM)] * 8,
         out_specs=(vmem, vmem),
         scratch_shapes=[
+            *[space(x.shape, x.dtype) for space, x in zip(spaces, operands)],
+            dma((len(operands),)),
             pltpu.VMEM(by_slot, BF16), pltpu.VMEM(by_slot, BF16),
             pltpu.VMEM(by_row, BF16), pltpu.VMEM(by_row, BF16),
             pltpu.VMEM(by_region, BF16), pltpu.VMEM(by_region, BF16),
@@ -281,25 +335,31 @@
             pltpu.VMEM((share, length, cells), F32),
             pltpu.VMEM((share, length, cells), F32),
             pltpu.VMEM((cells, cells), BF16), pltpu.VMEM((cells, cells), BF16),
-            pltpu.VMEM(by_region, F32), pltpu.VMEM(by_region, F32),
+            pltpu.VMEM(by_region, jnp.int16), pltpu.VMEM(by_region, F32),
+            pltpu.VMEM(by_row, jnp.int16),
+            pltpu.VMEM(by_slot, jnp.int16), pltpu.VMEM(by_slot, jnp.int16),
             pltpu.VMEM(by_row, F32),
-            pltpu.VMEM(by_slot, F32), pltpu.VMEM(by_slot, F32),
-            pltpu.VMEM(by_row, F32),
+            pltpu.VMEM((regions, share, LANES), F32), pltpu.VMEM((regions, share, LANES), F32),
+            pltpu.VMEM((groups, cap, LANES), F32), pltpu.VMEM((groups, cap, LANES), F32),
             dma((groups,)), dma((groups,)),
             dma((regions,)), dma((regions,)), dma((regions,)), dma((regions,)),
             dma((regions,)), dma((regions,)), dma((regions,)), dma((regions,)),
             dma((groups,)), dma((groups,)),
+            dma((regions,)), dma((regions,)), dma((groups,)), dma((groups,)),
         ],
         compiler_params=pltpu.CompilerParams(
             collective_id=0, has_side_effects=True, vmem_limit_bytes=32 * 1024 * 1024),
-    )(pairs, offsets, orbitals, *[jnp.asarray(t) for t in fixed_tables(length)])
-
-
-def collect_kernel(pairs, landed, home, out):
+    )(*[pltpu.with_memory_space_constraint(x, pltpu.HBM) for x in operands])
+
+
+def collect_kernel(pairs_in, landed, home, out, pairs, sem_in):
     groups, cap = landed.shape[:2]
     rows = home.shape[0]
     me = lax.axis_index("orb")
+    load = pltpu.make_async_copy(pairs_in, pairs, sem_in)
+    load.start()
     out[...] = jnp.zeros_like(out)
+    load.wait()
     for r in range(rows):
         k = pairs[0, me, r]
         out[k] += home[r]
@@ -311,14 +371,14 @@
 
 def collect(pairs, landed, home, shape):
     vmem = pl.BlockSpec(memory_space=pltpu.VMEM)
-    smem = pl.BlockSpec(memory_space=pltpu.SMEM)
     return pl.pallas_call(
         collect_kernel,
         out_shape=jax.ShapeDtypeStruct(shape, F32),
-        in_specs=[smem, vmem, vmem],
+        in_specs=[pl.BlockSpec(memory_space=pltpu.HBM), vmem, vmem],
         out_specs=vmem,
+        scratch_shapes=[pltpu.SMEM(pairs.shape, pairs.dtype), pltpu.SemaphoreType.DMA],
         compiler_params=pltpu.CompilerParams(vmem_limit_bytes=32 * 1024 * 1024),
-    )(pairs, landed, home)
+    )(pltpu.with_memory_space_constraint(pairs, pltpu.HBM), landed, home)
 
 
 def per_device(orbitals, pair_list, offsets):

time: 44.4 us -> 32.6 us (0.73)
  the two profiles are of different devices: /device:TPU:16 before, /device:TPU:0 now
where the time goes in v2:
time: 32.6 us; the launch traced here: 32.3 us
  Pallas kernels  32.3 us (99%)
    pallas_call x1, Pallas kernels, exchange_terms(): pl.pallas_call(exchange_kernel, out_shape=(jax.ShapeDtypeStruct(by_slot,...  29.9 us
    pallas_call x1, Pallas kernels, collect(): pl.pallas_call(collect_kernel, out_shape=jax.ShapeDtypeStruct(shape, F32)...  2.39 us

profile of v2, /device:TPU:0, one launch (start us, length us, event | category | flops | bytes accessed | tf_op | source)
XLA Modules:
  0.0 32.3 jit_solution(17456176149088510143)
XLA Ops:
  0.0 29.9 %shard_map.82 = (f32[8,2,8,1024]{3,2,1,0:T(8,128)S(1)}, f32[8,8,1024]{2,1,0:T(8,128)S(1)}) custom-call(s32[3,8,8]{2,1,0:T(8,128)} %bitcast.2, s32[3,512]{1,0:T(4,128)} %bitcast.4, bf16[64,8,1024]{2,1,0:T(8,128)(2,1)} %orbitals_in.1, f32[32,1024]{1,0:T(8,128)} %constant.10.clone.outer_in, f32[32,1024]{1,0:T(8,128)} %constant.11.clone.inner_in, ...), custom_call_target="tpu_custom_call" | custom-call | tf_op jit(solution)/shard_map/pallas_call | solution.py:323
  30.0 2.4 %shard_map.83 = f32[64,8,1024]{2,1,0:T(8,128)} custom-call(s32[3,8,8]{2,1,0:T(8,128)} %bitcast.3, f32[8,2,8,1024]{3,2,1,0:T(8,128)S(1)} %get-tuple-element.7.landed, f32[8,8,1024]{2,1,0:T(8,128)S(1)} %get-tuple-element.8.home), custom_call_target="tpu_custom_call" | custom-call | tf_op jit(solution)/shard_map/pallas_call | solution.py:374

commit v3 on v2

--- a/solution.py
+++ b/solution.py
@@ -32,12 +32,17 @@
     green = 1.0 / (
         levels[:, None, None] + levels[None, :, None] + levels[None, None, :] + SHIFT
     )
+    half = length // 2
+    parity = np.concatenate([np.arange(0, length, 2), np.arange(1, length, 2)])
     ones = np.ones((1, length))
+    near = [sine[:half, rows] for rows in (parity[:half], parity[half:])]
+    outer = np.stack([np.kron(part, ones) for part in (near[0], near[1], near[0].T, near[1].T)])
+    high, low = split_table(sine)
     return (
-        np.kron(sine, ones).astype(np.float32),
-        np.kron(ones, sine).astype(np.float32),
-        *split_table(sine),
-        green.reshape(length, length * length).astype(np.float32),
+        outer.astype(np.float32),
+        np.kron(np.ones((1, half)), sine).astype(np.float32),
+        np.concatenate([high, high, low], axis=1),
+        green[:, parity].reshape(length, length * length).astype(np.float32),
     )
 
 
@@ -81,9 +86,9 @@
 
 
 def exchange_kernel(
-    pairs_in, offsets_in, orbitals_in, outer_in, inner_in, sine_high_in, sine_low_in, green_in,
+    pairs_in, offsets_in, orbitals_in, outer_in, inner_in, sine_in, green_in,
     landed, home,
-    pairs, offsets, orbitals, outer, inner, sine_high, sine_low, green, sem_in,
+    pairs, offsets, orbitals, outer, inner, sine, green, sem_in,
     send_a, recv_a, stage_i, stage_j, box_i, box_j, field, shifted, second, plane_high, plane_low,
     term_i, term_j, rows_i, send_d, recv_d, rows_j, top_i, top_rows, send_top, recv_top,
     sem_sa, sem_ra, sem_si, sem_ri, sem_sj, sem_rj, sem_st, sem_rt, sem_su, sem_ru, sem_sd, sem_rd,
@@ -109,8 +114,7 @@
         pltpu.make_async_copy(source, target, sem_in.at[n])
         for n, (source, target) in enumerate((
             (pairs_in, pairs), (orbitals_in, orbitals), (offsets_in, offsets),
-            (outer_in, outer), (inner_in, inner), (green_in, green),
-            (sine_high_in, sine_high), (sine_low_in, sine_low)))
+            (outer_in, outer), (inner_in, inner), (green_in, green), (sine_in, sine)))
     ]
     for load in loads:
         load.start()
@@ -182,10 +186,14 @@
     for load in loads[2:]:
         load.wait()
 
-    @pl.loop(0, length)
+    half = length // 2
+
+    @pl.loop(0, half)
     def _(step):
         span = pl.ds(pl.multiple_of(step * length, length), length)
-        plane_high[span, :], plane_low[span, :] = split_field(outer[pl.ds(step, 1), :] * inner[...])
+        for n in range(4):
+            plane_high[n, span, :], plane_low[n, span, :] = split_field(
+                outer[n, pl.ds(step, 1), :] * inner[...])
 
     row = lax.broadcasted_iota(jnp.int32, (length, cells), 0)
     col = lax.broadcasted_iota(jnp.int32, (length, cells), 1)
@@ -233,21 +241,36 @@
             second[p, span, :] = box_i[part, p].astype(F32)
         field[p * length : (p + 1) * length, :] = second[p] * shifted[p]
 
-    def along_plane():
-        high, low = split_field(field[...])
-        field[...] = (
-            dot(high, plane_high[...]) + dot(low, plane_high[...]) + dot(high, plane_low[...])
-        )
+    flip = lax.rem(lax.broadcasted_iota(jnp.int32, (share * length, LANES), 1) // length, 2) == 0
+
+    def mirrored(values):
+        tiles = []
+        for n in range(values.shape[1] // LANES)[::-1]:
+            tile = values[:, n * LANES : (n + 1) * LANES]
+            tiles.append(jnp.where(flip, pltpu.roll(tile, length, 1), pltpu.roll(tile, LANES - length, 1)))
+        return jnp.concatenate(tiles, axis=1)
+
+    def product(values, n):
+        count = values.shape[0]
+        high, low = split_field(values)
+        both = dot(jnp.concatenate([high, low], axis=0), plane_high[n])
+        return both[:count] + both[count:] + dot(high, plane_low[n])
 
     def along_x(values):
         high, low = split_field(values)
-        return dot(sine_high[...], high) + dot(sine_high[...], low) + dot(sine_low[...], high)
-
-    along_plane()
+        return dot(sine[...], jnp.concatenate([high, low, high], axis=0))
+
+    middle = cells // 2
+    near, far = field[:, :middle], mirrored(field[:, middle:])
+    field[:, :middle] = product(near + far, 0)
+    field[:, middle:] = product(near - far, 1)
     for p in range(share):
         span = slice(p * length, (p + 1) * length)
         field[span, :] = along_x(along_x(field[span, :]) * green[...])
-    along_plane()
+    even = product(field[:, :middle], 2)
+    odd = product(field[:, middle:], 3)
+    field[:, :middle] = even + odd
+    field[:, middle:] = mirrored(even - odd)
     for p in range(share):
         code, top = encode(field[p * length : (p + 1) * length, :] * shifted[p])
         for part in range(regions):
@@ -262,7 +285,6 @@
         term = shift(field[p * length : (p + 1) * length, :] * second[p], *[-d for d in moves[p]])
         for part in range(regions):
             term_j[part, p] = term[part * depth : (part + 1) * depth, :]
-    copies += grp_send(*u_args)
     for p in range(share):
         rows_j[region * share + p] = term_j[region, p]
 
@@ -290,6 +312,8 @@
             copy = orb_copy(k, False, *args)
             copy.start()
             copies_a.append(copy)
+
+    copies += grp_send(*u_args)
 
     def arrived(source, codes, tops):
         for c in range(cap):
@@ -315,7 +339,7 @@
     vmem = pl.BlockSpec(memory_space=pltpu.VMEM)
     tables = [jnp.asarray(t) for t in fixed_tables(length)]
     operands = (pairs, offsets, orbitals, *tables)
-    spaces = [pltpu.SMEM, pltpu.SMEM] + [pltpu.VMEM] * 6
+    spaces = [pltpu.SMEM, pltpu.SMEM] + [pltpu.VMEM] * 5
     by_slot = (groups, cap, depth, cells)
     by_row = (rows, depth, cells)
     by_region = (regions, share, depth, cells)
@@ -323,7 +347,7 @@
     return pl.pallas_call(
         exchange_kernel,
         out_shape=(jax.ShapeDtypeStruct(by_slot, F32), jax.ShapeDtypeStruct(by_row, F32)),
-        in_specs=[pl.BlockSpec(memory_space=pltpu.HBM)] * 8,
+        in_specs=[pl.BlockSpec(memory_space=pltpu.HBM)] * 7,
         out_specs=(vmem, vmem),
         scratch_shapes=[
             *[space(x.shape, x.dtype) for space, x in zip(spaces, operands)],
@@ -334,7 +358,7 @@
             pltpu.VMEM((share * length, cells), F32),
             pltpu.VMEM((share, length, cells), F32),
             pltpu.VMEM((share, length, cells), F32),
-            pltpu.VMEM((cells, cells), BF16), pltpu.VMEM((cells, cells), BF16),
+            pltpu.VMEM((4, cells // 2, cells // 2), BF16), pltpu.VMEM((4, cells // 2, cells // 2), BF16),
             pltpu.VMEM(by_region, jnp.int16), pltpu.VMEM(by_region, F32),
             pltpu.VMEM(by_row, jnp.int16),
             pltpu.VMEM(by_slot, jnp.int16), pltpu.VMEM(by_slot, jnp.int16),

time: 32.6 us -> 30.6 us (0.939)
  Pallas kernels: 32.3 us -> 30.3 us
    pallas_call x1, Pallas kernels: 29.9 us -> 27.9 us  [exchange_terms(): pl.pallas_call(exchange_kernel, out_shape=(jax.ShapeDtypeStruct(by_slot,...]
where the time goes in v3:
time: 30.6 us; the launch traced here: 30.3 us
  Pallas kernels  30.3 us (99%)
    pallas_call x1, Pallas kernels, exchange_terms(): pl.pallas_call(exchange_kernel, out_shape=(jax.ShapeDtypeStruct(by_slot,...  27.9 us
    pallas_call x1, Pallas kernels, collect(): pl.pallas_call(collect_kernel, out_shape=jax.ShapeDtypeStruct(shape, F32)...  2.39 us

profile of v3, /device:TPU:0, one launch (start us, length us, event | category | flops | bytes accessed | tf_op | source)
XLA Modules:
  0.0 30.3 jit_solution(9402176936351537042)
XLA Ops:
  0.0 27.9 %shard_map.73 = (f32[8,2,8,1024]{3,2,1,0:T(8,128)S(1)}, f32[8,8,1024]{2,1,0:T(8,128)S(1)}) custom-call(s32[3,8,8]{2,1,0:T(8,128)} %bitcast.2, s32[3,512]{1,0:T(4,128)} %bitcast.4, bf16[64,8,1024]{2,1,0:T(8,128)(2,1)} %orbitals_in.1, f32[4,16,512]{2,1,0:T(8,128)} %constant.8.clone.outer_in, f32[32,512]{1,0:T(8,128)} %constant.9.clone.inner_in, ...), custom_call_target="tpu_custom_call" | custom-call | tf_op jit(solution)/shard_map/pallas_call | solution.py:347
  27.9 2.4 %shard_map.74 = f32[64,8,1024]{2,1,0:T(8,128)} custom-call(s32[3,8,8]{2,1,0:T(8,128)} %bitcast.3, f32[8,2,8,1024]{3,2,1,0:T(8,128)S(1)} %get-tuple-element.7.landed, f32[8,8,1024]{2,1,0:T(8,128)S(1)} %get-tuple-element.8.home), custom_call_target="tpu_custom_call" | custom-call | tf_op jit(solution)/shard_map/pallas_call | solution.py:398

commit v4 on v3

v4 whole, which is shorter than its diff:
```python
import math

import jax
import jax.numpy as jnp
import ml_dtypes
import numpy as np
from jax import lax
from jax.experimental import pallas as pl
from jax.experimental.pallas import tpu as pltpu
from jax.sharding import PartitionSpec as P

MESH = pl.DeviceIdType.MESH
SHIFT = 0.25
LANES = 128
F32 = jnp.float32
BF16 = jnp.bfloat16


def split_table(table):
    wide = np.asarray(table, np.float32)
    high = wide.astype(ml_dtypes.bfloat16)
    low = (wide - high.astype(np.float32)).astype(ml_dtypes.bfloat16)
    return high, low


def fixed_tables(length):
    counts = np.arange(length) + 1.0
    sine = np.sqrt(2.0 / (length + 1.0)) * np.sin(
        math.pi * counts[:, None] * counts[None, :] / (length + 1.0)
    )
    levels = 2.0 - 2.0 * np.cos(math.pi * counts / (length + 1.0))
    green = 1.0 / (
        levels[:, None, None] + levels[None, :, None] + levels[None, None, :] + SHIFT
    )
    half = length // 2
    parity = np.concatenate([np.arange(0, length, 2), np.arange(1, length, 2)])
    ones = np.ones((1, length))
    near = [sine[:half, rows] for rows in (parity[:half], parity[half:])]
    outer = np.stack([np.kron(part, ones) for part in (near[0], near[1], near[0].T, near[1].T)])
    high, low = split_table(sine)
    width = half * length
    inner = np.kron(np.ones((1, half)), sine)
    wide = np.zeros((length, width))
    wide[:, : 3 * length] = np.concatenate([high, high, low], axis=1).astype(np.float32)
    green = green[:, parity].reshape(length, 2 * width)
    return np.concatenate(
        [outer.reshape(4 * half, width), inner, wide, green[:, :width], green[:, width:]]
    ).astype(np.float32)


def split_field(field):
    high = field.astype(BF16)
    return high, (field - high.astype(F32)).astype(BF16)


def dot(left, right):
    return jnp.dot(left, right, preferred_element_type=F32)


def grp_order(count):
    return sorted(range(1, count), key=lambda k: -min(k, count - k))


def slot_order(groups, cap, regions, rows):
    far = list(range(groups))[::-1]
    share = rows // regions
    needed = [((b + 1) * regions - 1 + groups * cap - rows) // cap + 1 for b in range(share)]
    closed = [(b + 1) * regions // cap for b in range(share - 1)] + [groups]
    late, early = groups - needed[0], closed[0]
    order = far[:early] + far[early + late :] + far[early : early + late]
    return order, needed, closed


def partner(index, offset):
    value, bit = index, 1
    while bit <= offset:
        if offset & bit:
            value = value + bit - 2 * bit * lax.rem(lax.div(index, bit), 2)
        bit *= 2
    return value


def find(pairs, block, wanted, what, rows):
    value = jnp.int32(0)
    valid = jnp.int32(0)
    for r in range(rows):
        hit = pairs[2, block, r] == wanted
        value = jnp.where(hit, what(r), value)
        valid = jnp.where(hit, jnp.int32(1), valid)
    return value, valid


LEVELS = 32766.0


def encode(values):
    size = jnp.abs(values)
    top = jnp.maximum(jnp.max(jnp.max(size, axis=0, keepdims=True), axis=1, keepdims=True), 1e-36)
    steps = (jnp.sqrt(size * (1.0 / top)) * LEVELS + 0.5).astype(jnp.int32)
    code = jnp.where(values < 0.0, -steps, steps).astype(jnp.int16)
    return code, jnp.broadcast_to(top, (1, LANES))


def decode(code, top):
    steps = code.astype(jnp.int32).astype(F32)
    return steps * jnp.abs(steps) * (top[:, 0:1] * (1.0 / (LEVELS * LEVELS)))


def exchange_kernel(
    pairs_in, offsets_in, orbitals_in, tables_in,
    landed, home,
    pairs, offsets, orbitals, tables, sem_in,
    send_a, recv_a, slots_a, stage_i, stage_j, box_i, box_j, field, shifted, second,
    plane_high, plane_low, term_i, term_j, rows_i, every_i, rows_j, top_i, top_rows, every_top,
    send_d, recv_d, send_top, recv_top,
    sem_sa, sem_ra, sem_si, sem_ri, sem_sj, sem_rj, sem_st, sem_rt, sem_su, sem_ru, sem_sd, sem_rd,
    sem_sv, sem_rv, sem_sw, sem_rw,
):
    groups, cap, depth, cells = send_a.shape
    share, regions = box_i.shape[:2]
    rows = regions * share
    length = regions * depth
    local_count = orbitals.shape[0]
    me = lax.axis_index("orb")
    region = lax.axis_index("grp")
    grp_steps = grp_order(regions)
    order, needed, closed = slot_order(groups, cap, regions, rows)
    batches = range(share)
    begun = []

    def grp_peer(k):
        return lax.rem(region + k, regions)

    def other(n):
        return partner(me, order[n])

    loads = [
        pltpu.make_async_copy(source, target, sem_in.at[n])
        for n, (source, target) in enumerate((
            (pairs_in, pairs), (orbitals_in, orbitals), (offsets_in, offsets),
            (tables_in, tables)))
    ]
    for load in loads:
        load.start()
    barrier = pltpu.get_barrier_semaphore()
    for k in range(1, groups):
        pl.semaphore_signal(
            barrier, inc=1, device_id={"orb": lax.rem(me + k, groups)}, device_id_type=MESH)
    for k in grp_steps:
        pl.semaphore_signal(barrier, inc=1, device_id={"grp": grp_peer(k)}, device_id_type=MESH)
    loads[0].wait()

    places = []
    for r in range(rows):
        slot = pairs[2, me, r]
        group = lax.div(slot, cap)
        place = jnp.int32(0)
        for n in range(groups):
            place = jnp.where(group == other(n), jnp.int32(n * cap), place)
        places.append(place + lax.rem(slot, cap))
    ranks = []
    for r in range(rows):
        rank = jnp.int32(0)
        for q in range(rows):
            if q != r:
                rank = rank + jnp.where(places[q] < places[r], jnp.int32(1), jnp.int32(0))
        ranks.append(rank)

    def ranked(values, rank):
        value = jnp.int32(0)
        for r in range(rows):
            value = jnp.where(ranks[r] == rank, values[r], value)
        return value

    row_of = [ranked([jnp.int32(r) for r in range(rows)], q) for q in range(rows)]
    place_of = [ranked(places, q) for q in range(rows)]

    asked = []
    for n in range(groups):
        block = other(n)
        for c in range(cap):
            asked.append(find(pairs, block, me * cap + c, lambda r: pairs[1, block, r], rows)[0])
    loads[1].wait()
    for n in range(groups):
        for c in range(cap):
            send_a[n, c] = orbitals[asked[n * cap + c]]
    for b in batches:
        for part in range(regions):
            stage_j[part, b] = orbitals[pairs[0, me, row_of[b * regions + part]]]
    pl.semaphore_wait(barrier, groups + regions - 2)

    def orb_copy(n, source, target, send_sem, recv_sem):
        return pltpu.make_async_remote_copy(
            src_ref=source, dst_ref=target, send_sem=send_sem, recv_sem=recv_sem,
            device_id={"orb": other(n)}, device_id_type=MESH)

    def bytes_of(ref, sem):
        return pltpu.make_async_copy(ref, ref, sem)

    def grp_send(source, target, send_sem, recv_sem):
        for k in grp_steps:
            peer = grp_peer(k)
            pltpu.make_async_remote_copy(
                src_ref=source.at[peer], dst_ref=target.at[region],
                send_sem=send_sem, recv_sem=recv_sem,
                device_id={"grp": peer}, device_id_type=MESH).start()
        begun.append(bytes_of(source.at[pl.ds(0, regions - 1)], send_sem))

    def grp_wait(source, target, send_sem, recv_sem):
        bytes_of(target.at[pl.ds(0, regions - 1)], recv_sem).wait()

    j_args = (stage_j, box_j, sem_sj.at[0], sem_rj.at[0])
    i_args = [(stage_i.at[b], box_i.at[b], sem_si.at[b], sem_ri.at[b]) for b in batches]
    t_args = [(term_i.at[b], rows_i[b], sem_st.at[b], sem_rt.at[b]) for b in batches]
    v_args = [(top_i.at[b], top_rows[b], sem_sv.at[b], sem_rv.at[b]) for b in batches]
    u_args = [(term_j.at[b], rows_j.at[b], sem_su.at[b], sem_ru.at[b]) for b in batches]

    spans = [range(needed[b - 1] if b else 0, needed[b]) for b in batches]

    def box_copy(b, n):
        return orb_copy(n, send_a.at[n], recv_a[b].at[n - spans[b][0]], sem_sa.at[0], sem_ra.at[b])

    for b in batches:
        for n in spans[b]:
            if order[n]:
                box_copy(b, n).start()
    begun.append(bytes_of(send_a.at[pl.ds(0, groups - 1)], sem_sa.at[0]))
    grp_send(*j_args)
    for b in batches:
        for n in spans[b]:
            if not order[n]:
                for c in range(cap):
                    recv_a[b][n - spans[b][0], c] = send_a[n, c]
    box_j[region] = stage_j[region]

    for load in loads[2:]:
        load.wait()
    half = length // 2
    inner, wide, near, far = [
        slice(4 * half + n * length, 4 * half + (n + 1) * length) for n in range(4)]

    @pl.loop(0, half)
    def _(step):
        span = pl.ds(pl.multiple_of(step * length, length), length)
        for n in range(4):
            plane_high[n, span, :], plane_low[n, span, :] = split_field(
                tables[pl.ds(n * half + step, 1), :] * tables[inner, :])

    sine = tables[wide, : 3 * length].astype(BF16)
    green = jnp.concatenate([tables[near, :], tables[far, :]], axis=1)

    row = lax.broadcasted_iota(jnp.int32, (length, cells), 0)
    col = lax.broadcasted_iota(jnp.int32, (length, cells), 1)
    mid = col // length
    last = col - mid * length
    flip = lax.rem(lax.broadcasted_iota(jnp.int32, (length, LANES), 1) // length, 2) == 0

    def shift(values, dx, dy, dz):
        moved = pltpu.roll(values, jnp.remainder(-dx + length, length), 0)
        flat = jnp.remainder(2 * cells - dy * length - dz, cells)
        moved = pltpu.roll(moved, flat, 1)
        x, y, z = row + dx, mid + dy, last + dz
        keep = (x >= 0) & (x < length) & (y >= 0) & (y < length) & (z >= 0) & (z < length)
        return jnp.where(keep, moved, 0.0)

    def mirrored(values):
        tiles = []
        for n in range(values.shape[1] // LANES)[::-1]:
            tile = values[:, n * LANES : (n + 1) * LANES]
            tiles.append(jnp.where(flip, pltpu.roll(tile, length, 1), pltpu.roll(tile, LANES - length, 1)))
        return jnp.concatenate(tiles, axis=1)

    def product(values, n):
        count = values.shape[0]
        high, low = split_field(values)
        both = dot(jnp.concatenate([high, low], axis=0), plane_high[n])
        return both[:count] + both[count:] + dot(high, plane_low[n])

    def along_x(values):
        high, low = split_field(values)
        return dot(sine, jnp.concatenate([high, low, high], axis=0))

    def whole(box, b):
        for part in range(regions):
            field[b, part * depth : (part + 1) * depth, :] = box(part).astype(F32)
        return field[b]

    moves = []
    for b in batches:
        r = jnp.int32(0)
        for part in range(regions):
            r = jnp.where(region == part, row_of[b * regions + part], r)
        j = me * local_count + pairs[0, me, r]
        i = lax.div(pairs[2, me, r], cap) * local_count + pairs[1, me, r]
        moves.append([offsets[a, j] - offsets[a, i] for a in range(3)])

    grp_wait(*j_args)
    for b in batches:
        shifted[b] = shift(whole(lambda part: box_j[part, b], b), *moves[b])

    for b in batches:
        away = sum(order[n] > 0 for n in spans[b])
        bytes_of(recv_a[b].at[pl.ds(0, away)], sem_ra.at[b]).wait()
        for n in spans[b]:
            for c in range(cap):
                slots_a[b][n * cap + c] = recv_a[b][n - spans[b][0], c]
        for part in range(regions):
            place = jnp.minimum(place_of[b * regions + part], needed[b] * cap - 1)
            stage_i[b, part] = slots_a[b][place]
        grp_send(*i_args[b])
        box_i[b, region] = stage_i[b, region]
        if b + 1 < share:
            for n in range(needed[b] * cap):
                slots_a[b + 1][n] = slots_a[b][n]

    middle = cells // 2
    for b in batches:
        grp_wait(*i_args[b])
        second[b] = whole(lambda part: box_i[b, part], b)
        charge = second[b] * shifted[b]
        left, right = charge[:, :middle], mirrored(charge[:, middle:])
        field[b, :, :middle] = product(left + right, 0)
        field[b, :, middle:] = product(left - right, 1)
        field[b] = along_x(along_x(field[b]) * green)
        even = product(field[b, :, :middle], 2)
        odd = product(field[b, :, middle:], 3)
        field[b, :, :middle] = even + odd
        field[b, :, middle:] = mirrored(even - odd)
        code, top = encode(field[b] * shifted[b])
        for part in range(regions):
            term_i[b, part] = code[part * depth : (part + 1) * depth, :]
            top_i[b, part] = top
        grp_send(*t_args[b])
        grp_send(*v_args[b])
        rows_i[b][region] = term_i[b, region]
        top_rows[b][region] = top_i[b, region]

    for b in batches:
        term = shift(field[b] * second[b], *[-d for d in moves[b]])
        for part in range(regions):
            term_j[b, part] = term[part * depth : (part + 1) * depth, :]
        rows_j[b, region] = term_j[b, region]

    def term_copies(b, n):
        return (
            orb_copy(n, send_top.at[n], recv_top.at[n], sem_sw.at[0], sem_rw.at[b]),
            orb_copy(n, send_d.at[n], recv_d.at[n], sem_sd.at[0], sem_rd.at[n]),
        )

    sends = []
    for b in batches:
        grp_wait(*t_args[b])
        grp_wait(*v_args[b])
        for part in range(regions):
            for later in range(b, share):
                every_i[later][b * regions + part] = rows_i[b][part]
                every_top[later][b * regions + part] = top_rows[b][part]
        leaving = range(closed[b - 1] if b else 0, closed[b])
        leaving = sorted(leaving, key=lambda n: -order[n])
        for n in leaving:
            for c in range(cap):
                q, _ = find(pairs, me, other(n) * cap + c, lambda r: ranks[r], rows)
                q = jnp.minimum(q, (b + 1) * regions - 1)
                send_d[n, c] = every_i[b][q]
                send_top[n, c : c + 1] = every_top[b][q]
        for n in leaving:
            if order[n]:
                for copy in term_copies(b, n):
                    copy.start()
        sends.append([n for n in leaving if order[n]])
        if b == 0:
            for args in u_args:
                grp_send(*args)

    def arrived(n, codes, tops):
        for c in range(cap):
            landed[n, c] = decode(codes[n, c], tops[n, c : c + 1])

    for n in range(groups):
        if not order[n]:
            arrived(n, send_d, send_top)
    for args in u_args:
        grp_wait(*args)
    for r in range(rows):
        home[r] = rows_j[lax.div(ranks[r], regions), lax.rem(ranks[r], regions)]
    for b in batches:
        bytes_of(recv_top.at[pl.ds(0, len(sends[b]))], sem_rw.at[b]).wait()
        for n in sends[b]:
            bytes_of(recv_d.at[n], sem_rd.at[n]).wait()
            arrived(n, recv_d, recv_top)
    begun.append(bytes_of(send_top.at[pl.ds(0, groups - 1)], sem_sw.at[0]))
    begun.append(bytes_of(send_d.at[pl.ds(0, groups - 1)], sem_sd.at[0]))
    for copy in begun:
        copy.wait()


def exchange_terms(pairs, offsets, orbitals, groups, regions):
    _, depth, cells = orbitals.shape
    rows = pairs.shape[2]
    share = rows // regions
    cap = 2 * rows // groups
    length = depth * regions
    vmem = pl.BlockSpec(memory_space=pltpu.VMEM)
    operands = (pairs, offsets, orbitals, jnp.asarray(fixed_tables(length)))
    spaces = [pltpu.SMEM, pltpu.SMEM, pltpu.VMEM, pltpu.VMEM]
    by_slot = (groups, cap, depth, cells)
    by_batch = (share, regions, depth, cells)
    by_region = (regions, depth, cells)
    dma = pltpu.SemaphoreType.DMA
    one, each, orb_sem = dma((1,)), dma((share,)), dma((groups,))
    _, needed, _ = slot_order(groups, cap, regions, rows)
    parts = [last - first for first, last in zip([0] + needed[:-1], needed)]
    box = (length, cells)
    table = (4, cells // 2, cells // 2)
    i16 = jnp.int16
    return pl.pallas_call(
        exchange_kernel,
        out_shape=(
            jax.ShapeDtypeStruct(by_slot, F32), jax.ShapeDtypeStruct((rows, depth, cells), F32)),
        in_specs=[pl.BlockSpec(memory_space=pltpu.HBM)] * len(operands),
        out_specs=(vmem, vmem),
        scratch_shapes=[
            *[space(x.shape, x.dtype) for space, x in zip(spaces, operands)],
            dma((len(operands),)),
            pltpu.VMEM(by_slot, BF16),
            [pltpu.VMEM((count, cap, depth, cells), BF16) for count in parts],
            [pltpu.VMEM((count * cap, depth, cells), BF16) for count in needed],
            pltpu.VMEM(by_batch, BF16),
            pltpu.VMEM((regions, share, depth, cells), BF16),
            pltpu.VMEM(by_batch, BF16),
            pltpu.VMEM((regions, share, depth, cells), BF16),
            pltpu.VMEM((share, *box), F32), pltpu.VMEM((share, *box), F32),
            pltpu.VMEM((share, *box), F32),
            pltpu.VMEM(table, BF16), pltpu.VMEM(table, BF16),
            pltpu.VMEM(by_batch, i16), pltpu.VMEM(by_batch, F32),
            [pltpu.VMEM(by_region, i16) for _ in range(share)],
            [pltpu.VMEM(((b + 1) * regions, depth, cells), i16) for b in range(share)],
            pltpu.VMEM(by_batch, F32),
            pltpu.VMEM((share, regions, 1, LANES), F32),
            [pltpu.VMEM((regions, 1, LANES), F32) for _ in range(share)],
            [pltpu.VMEM(((b + 1) * regions, 1, LANES), F32) for b in range(share)],
            pltpu.VMEM(by_slot, i16), pltpu.VMEM(by_slot, i16),
            pltpu.VMEM((groups, cap, LANES), F32), pltpu.VMEM((groups, cap, LANES), F32),
            one, each, each, each, one, one, each, each, each, each, one, orb_sem,
            each, each, one, each,
        ],
        compiler_params=pltpu.CompilerParams(
            collective_id=0, has_side_effects=True, vmem_limit_bytes=32 * 1024 * 1024),
    )(*[pltpu.with_memory_space_constraint(x, pltpu.HBM) for x in operands])


def collect_kernel(pairs_in, landed, home, out, pairs, sem_in):
    groups, cap = landed.shape[:2]
    rows = home.shape[0]
    order, _, _ = slot_order(groups, cap, lax.axis_size("grp"), rows)
    me = lax.axis_index("orb")
    load = pltpu.make_async_copy(pairs_in, pairs, sem_in)
    load.start()
    out[...] = jnp.zeros_like(out)
    load.wait()
    for r in range(rows):
        k = pairs[0, me, r]
        out[k] += home[r]
    for n in range(groups):
        block = partner(me, order[n])
        for c in range(cap):
            k, valid = find(pairs, block, me * cap + c, lambda r: pairs[1, block, r], rows)
            out[k] += jnp.where(valid > 0, landed[n, c], 0.0)


def collect(pairs, landed, home, shape):
    vmem = pl.BlockSpec(memory_space=pltpu.VMEM)
    return pl.pallas_call(
        collect_kernel,
        out_shape=jax.ShapeDtypeStruct(shape, F32),
        in_specs=[pl.BlockSpec(memory_space=pltpu.HBM), vmem, vmem],
        out_specs=vmem,
        scratch_shapes=[pltpu.SMEM(pairs.shape, pairs.dtype), pltpu.SemaphoreType.DMA],
        compiler_params=pltpu.CompilerParams(vmem_limit_bytes=32 * 1024 * 1024),
    )(pltpu.with_memory_space_constraint(pairs, pltpu.HBM), landed, home)


def per_device(orbitals, pair_list, offsets):
    groups = lax.axis_size("orb")
    regions = lax.axis_size("grp")
    pairs = jnp.transpose(pair_list, (2, 0, 1))
    landed, home = exchange_terms(pairs, offsets.T, orbitals, groups, regions)
    return collect(pairs, landed, home, orbitals.shape)


def solution(mesh):
    in_specs = (P("orb", "grp", None), P(), P())
    out_specs = P("orb", "grp", None)
    return jax.shard_map(
        per_device, mesh=mesh, in_specs=in_specs, out_specs=out_specs, check_vma=False
    )
```

time: 30.6 us -> 28.9 us (0.944)
  Pallas kernels: 30.3 us -> 28.6 us
    pallas_call x1, Pallas kernels: 27.9 us -> 26.1 us  [exchange_terms(): pl.pallas_call(exchange_kernel, out_shape=(jax.ShapeDtypeStruct(by_slot,...]
where the time goes in v4:
time: 28.9 us; the launch traced here: 28.6 us
  Pallas kernels  28.6 us (99%)
    pallas_call x1, Pallas kernels, exchange_terms(): pl.pallas_call(exchange_kernel, out_shape=(jax.ShapeDtypeStruct(by_slot,...  26.1 us
    pallas_call x1, Pallas kernels, collect(): pl.pallas_call(collect_kernel, out_shape=jax.ShapeDtypeStruct(shape, F32)...  2.46 us

profile of v4, /device:TPU:0, one launch (start us, length us, event | category | flops | bytes accessed | tf_op | source)
XLA Modules:
  0.0 28.6 jit_solution(2182433456024735847)
XLA Ops:
  0.0 26.1 %shard_map.46 = (f32[8,2,8,1024]{3,2,1,0:T(8,128)S(1)}, f32[8,8,1024]{2,1,0:T(8,128)S(1)}) custom-call(s32[3,8,8]{2,1,0:T(8,128)} %bitcast.2, s32[3,512]{1,0:T(4,128)} %bitcast.4, bf16[64,8,1024]{2,1,0:T(8,128)(2,1)} %orbitals_in.1, f32[192,512]{1,0:T(8,128)} %constant.2.clone.tables_in), custom_call_target="tpu_custom_call" | custom-call | tf_op jit(solution)/shard_map/pallas_call | solution.py:416
  26.1 2.5 %shard_map.47 = f32[64,8,1024]{2,1,0:T(8,128)} custom-call(s32[3,8,8]{2,1,0:T(8,128)} %bitcast.3, f32[8,2,8,1024]{3,2,1,0:T(8,128)S(1)} %get-tuple-element.7.landed, f32[8,8,1024]{2,1,0:T(8,128)S(1)} %get-tuple-element.8.home), custom_call_target="tpu_custom_call" | custom-call | tf_op jit(solution)/shard_map/pallas_call | solution.py:473

commit v5 on v4

--- a/solution.py
+++ b/solution.py
@@ -33,19 +33,24 @@
         levels[:, None, None] + levels[None, :, None] + levels[None, None, :] + SHIFT
     )
     half = length // 2
-    parity = np.concatenate([np.arange(0, length, 2), np.arange(1, length, 2)])
-    ones = np.ones((1, length))
-    near = [sine[:half, rows] for rows in (parity[:half], parity[half:])]
-    outer = np.stack([np.kron(part, ones) for part in (near[0], near[1], near[0].T, near[1].T)])
     high, low = split_table(sine)
-    width = half * length
-    inner = np.kron(np.ones((1, half)), sine)
-    wide = np.zeros((length, width))
-    wide[:, : 3 * length] = np.concatenate([high, high, low], axis=1).astype(np.float32)
-    green = green[:, parity].reshape(length, 2 * width)
-    return np.concatenate(
-        [outer.reshape(4 * half, width), inner, wide, green[:, :width], green[:, width:]]
-    ).astype(np.float32)
+    lane = np.arange(half * half)
+    inner = lane % length
+    mirror = inner >= half
+    y = (lane // LANES * 2 + mirror) * (LANES // length) + lane % LANES // length
+    z = np.where(mirror, length - 1 - inner, inner)
+    tables, greens = [], []
+    for odd_y in (0, 1):
+        for odd_z in (0, 1):
+            b, c = 2 * (lane // half) + odd_y, 2 * (lane % half) + odd_z
+            table = sine[y[:, None], b] * sine[z[:, None], c]
+            sign = np.where(mirror & (odd_z == 1), -1.0, 1.0)
+            tables += [*split_table(table * sign[:, None]), *split_table(table.T)]
+            greens.append(green[:, b, c])
+    small = np.concatenate(greens + [np.zeros((length, LANES))], axis=1).astype(np.float32)
+    small[:, length * length : length * length + 3 * length] = np.concatenate(
+        [high, high, low], axis=1)
+    return np.stack(tables), small
 
 
 def split_field(field):
@@ -107,11 +112,11 @@
 
 
 def exchange_kernel(
-    pairs_in, offsets_in, orbitals_in, tables_in,
-    landed, home,
-    pairs, offsets, orbitals, tables, sem_in,
+    pairs_in, offsets_in, orbitals_in, tables_in, small_in,
+    landed, home, targets,
+    pairs, offsets, orbitals, tables, small, sem_in,
     send_a, recv_a, slots_a, stage_i, stage_j, box_i, box_j, field, shifted, second,
-    plane_high, plane_low, term_i, term_j, rows_i, every_i, rows_j, top_i, top_rows, every_top,
+    term_i, term_j, rows_i, every_i, rows_j, top_i, top_rows, every_top,
     send_d, recv_d, send_top, recv_top,
     sem_sa, sem_ra, sem_si, sem_ri, sem_sj, sem_rj, sem_st, sem_rt, sem_su, sem_ru, sem_sd, sem_rd,
     sem_sv, sem_rv, sem_sw, sem_rw,
@@ -138,7 +143,7 @@
         pltpu.make_async_copy(source, target, sem_in.at[n])
         for n, (source, target) in enumerate((
             (pairs_in, pairs), (orbitals_in, orbitals), (offsets_in, offsets),
-            (tables_in, tables)))
+            (tables_in, tables), (small_in, small)))
     ]
     for load in loads:
         load.start()
@@ -150,6 +155,53 @@
         pl.semaphore_signal(barrier, inc=1, device_id={"grp": grp_peer(k)}, device_id_type=MESH)
     loads[0].wait()
 
+    asked = []
+    for n in range(groups):
+        block = other(n)
+        for c in range(cap):
+            asked.append(find(pairs, block, me * cap + c, lambda r: pairs[1, block, r], rows))
+    loads[1].wait()
+    for n in range(groups):
+        for c in range(cap):
+            send_a[n, c] = orbitals[asked[n * cap + c][0]]
+    pl.semaphore_wait(barrier, groups + regions - 2)
+
+    def orb_copy(n, source, target, send_sem, recv_sem):
+        return pltpu.make_async_remote_copy(
+            src_ref=source, dst_ref=target, send_sem=send_sem, recv_sem=recv_sem,
+            device_id={"orb": other(n)}, device_id_type=MESH)
+
+    def bytes_of(ref, sem):
+        return pltpu.make_async_copy(ref, ref, sem)
+
+    def grp_send(source, target, send_sem, recv_sem):
+        for k in grp_steps:
+            peer = grp_peer(k)
+            pltpu.make_async_remote_copy(
+                src_ref=source.at[peer], dst_ref=target.at[region],
+                send_sem=send_sem, recv_sem=recv_sem,
+                device_id={"grp": peer}, device_id_type=MESH).start()
+        begun.append(bytes_of(source.at[pl.ds(0, regions - 1)], send_sem))
+
+    def grp_wait(source, target, send_sem, recv_sem):
+        bytes_of(target.at[pl.ds(0, regions - 1)], recv_sem).wait()
+
+    j_args = (stage_j, box_j, sem_sj.at[0], sem_rj.at[0])
+    i_args = [(stage_i.at[b], box_i.at[b], sem_si.at[b], sem_ri.at[b]) for b in batches]
+    t_args = [(term_i.at[b], rows_i[b], sem_st.at[b], sem_rt.at[b]) for b in batches]
+    v_args = [(top_i.at[b], top_rows[b], sem_sv.at[b], sem_rv.at[b]) for b in batches]
+    u_args = [(term_j.at[b], rows_j.at[b], sem_su.at[b], sem_ru.at[b]) for b in batches]
+
+    spans = [range(needed[b - 1] if b else 0, needed[b]) for b in batches]
+
+    def box_copy(b, n):
+        return orb_copy(n, send_a.at[n], recv_a[b].at[n - spans[b][0]], sem_sa.at[0], sem_ra.at[b])
+
+    for b in batches:
+        for n in spans[b]:
+            if order[n]:
+                box_copy(b, n).start()
+    begun.append(bytes_of(send_a.at[pl.ds(0, groups - 1)], sem_sa.at[0]))
     places = []
     for r in range(rows):
         slot = pairs[2, me, r]
@@ -175,56 +227,9 @@
     row_of = [ranked([jnp.int32(r) for r in range(rows)], q) for q in range(rows)]
     place_of = [ranked(places, q) for q in range(rows)]
 
-    asked = []
-    for n in range(groups):
-        block = other(n)
-        for c in range(cap):
-            asked.append(find(pairs, block, me * cap + c, lambda r: pairs[1, block, r], rows)[0])
-    loads[1].wait()
-    for n in range(groups):
-        for c in range(cap):
-            send_a[n, c] = orbitals[asked[n * cap + c]]
     for b in batches:
         for part in range(regions):
             stage_j[part, b] = orbitals[pairs[0, me, row_of[b * regions + part]]]
-    pl.semaphore_wait(barrier, groups + regions - 2)
-
-    def orb_copy(n, source, target, send_sem, recv_sem):
-        return pltpu.make_async_remote_copy(
-            src_ref=source, dst_ref=target, send_sem=send_sem, recv_sem=recv_sem,
-            device_id={"orb": other(n)}, device_id_type=MESH)
-
-    def bytes_of(ref, sem):
-        return pltpu.make_async_copy(ref, ref, sem)
-
-    def grp_send(source, target, send_sem, recv_sem):
-        for k in grp_steps:
-            peer = grp_peer(k)
-            pltpu.make_async_remote_copy(
-                src_ref=source.at[peer], dst_ref=target.at[region],
-                send_sem=send_sem, recv_sem=recv_sem,
-                device_id={"grp": peer}, device_id_type=MESH).start()
-        begun.append(bytes_of(source.at[pl.ds(0, regions - 1)], send_sem))
-
-    def grp_wait(source, target, send_sem, recv_sem):
-        bytes_of(target.at[pl.ds(0, regions - 1)], recv_sem).wait()
-
-    j_args = (stage_j, box_j, sem_sj.at[0], sem_rj.at[0])
-    i_args = [(stage_i.at[b], box_i.at[b], sem_si.at[b], sem_ri.at[b]) for b in batches]
-    t_args = [(term_i.at[b], rows_i[b], sem_st.at[b], sem_rt.at[b]) for b in batches]
-    v_args = [(top_i.at[b], top_rows[b], sem_sv.at[b], sem_rv.at[b]) for b in batches]
-    u_args = [(term_j.at[b], rows_j.at[b], sem_su.at[b], sem_ru.at[b]) for b in batches]
-
-    spans = [range(needed[b - 1] if b else 0, needed[b]) for b in batches]
-
-    def box_copy(b, n):
-        return orb_copy(n, send_a.at[n], recv_a[b].at[n - spans[b][0]], sem_sa.at[0], sem_ra.at[b])
-
-    for b in batches:
-        for n in spans[b]:
-            if order[n]:
-                box_copy(b, n).start()
-    begun.append(bytes_of(send_a.at[pl.ds(0, groups - 1)], sem_sa.at[0]))
     grp_send(*j_args)
     for b in batches:
         for n in spans[b]:
@@ -233,27 +238,26 @@
                     recv_a[b][n - spans[b][0], c] = send_a[n, c]
     box_j[region] = stage_j[region]
 
+    for n, (local, valid) in enumerate(asked):
+        targets[0, n] = local
+        targets[1, n] = valid
+    for r in range(rows):
+        targets[2, r] = pairs[0, me, r]
+
     for load in loads[2:]:
         load.wait()
-    half = length // 2
-    inner, wide, near, far = [
-        slice(4 * half + n * length, 4 * half + (n + 1) * length) for n in range(4)]
-
-    @pl.loop(0, half)
-    def _(step):
-        span = pl.ds(pl.multiple_of(step * length, length), length)
-        for n in range(4):
-            plane_high[n, span, :], plane_low[n, span, :] = split_field(
-                tables[pl.ds(n * half + step, 1), :] * tables[inner, :])
-
-    sine = tables[wide, : 3 * length].astype(BF16)
-    green = jnp.concatenate([tables[near, :], tables[far, :]], axis=1)
+    sine = small[:, cells : cells + 3 * length].astype(BF16)
+    green = small[:, :cells]
 
     row = lax.broadcasted_iota(jnp.int32, (length, cells), 0)
     col = lax.broadcasted_iota(jnp.int32, (length, cells), 1)
     mid = col // length
     last = col - mid * length
-    flip = lax.rem(lax.broadcasted_iota(jnp.int32, (length, LANES), 1) // length, 2) == 0
+    lane = lax.broadcasted_iota(jnp.int32, (length, LANES), 1)
+    inner = lax.rem(lane, length)
+    near = inner < length // 2
+    flip_y = LANES - length - lane + 2 * inner
+    flip_z = lane + length - 1 - 2 * inner
 
     def shift(values, dx, dy, dz):
         moved = pltpu.roll(values, jnp.remainder(-dx + length, length), 0)
@@ -263,18 +267,46 @@
         keep = (x >= 0) & (x < length) & (y >= 0) & (y < length) & (z >= 0) & (z < length)
         return jnp.where(keep, moved, 0.0)
 
-    def mirrored(values):
-        tiles = []
-        for n in range(values.shape[1] // LANES)[::-1]:
-            tile = values[:, n * LANES : (n + 1) * LANES]
-            tiles.append(jnp.where(flip, pltpu.roll(tile, length, 1), pltpu.roll(tile, LANES - length, 1)))
+    def taken(tile, index):
+        return jnp.take_along_axis(tile, index, axis=1)
+
+    def joined(tiles):
         return jnp.concatenate(tiles, axis=1)
+
+    def folded(values):
+        count = cells // LANES
+        tiles = [values[:, n * LANES : (n + 1) * LANES] for n in range(count)]
+        far = [taken(tiles[count - 1 - n], flip_y) for n in range(count // 2)]
+        quarters = []
+        for side in (1.0, -1.0):
+            half = [tile + other if side > 0 else tile - other for tile, other in zip(tiles, far)]
+            back = [taken(tile, flip_z) for tile in half]
+            even = [tile + other for tile, other in zip(half, back)]
+            odd = [tile - other for tile, other in zip(half, back)]
+            for part in (even, odd):
+                quarters.append(joined(
+                    [jnp.where(near, part[n], part[n + 1]) for n in range(0, count // 2, 2)]))
+        return quarters
+
+    def unfolded(quarters):
+        count = cells // LANES
+        halves = []
+        for even, odd in (quarters[:2], quarters[2:]):
+            total, rest = even + odd, even - odd
+            tiles = []
+            for n in range(count // 4):
+                here = slice(n * LANES, (n + 1) * LANES)
+                tiles.append(jnp.where(near, total[:, here], taken(rest[:, here], flip_z)))
+                tiles.append(jnp.where(near, taken(total[:, here], flip_z), rest[:, here]))
+            halves.append(tiles)
+        first = [even + odd for even, odd in zip(*halves)]
+        return joined(first + [taken(even - odd, flip_y) for even, odd in zip(*halves)][::-1])
 
     def product(values, n):
         count = values.shape[0]
         high, low = split_field(values)
-        both = dot(jnp.concatenate([high, low], axis=0), plane_high[n])
-        return both[:count] + both[count:] + dot(high, plane_low[n])
+        both = dot(jnp.concatenate([high, low], axis=0), tables[2 * n])
+        return both[:count] + both[count:] + dot(high, tables[2 * n + 1])
 
     def along_x(values):
         high, low = split_field(values)
@@ -313,19 +345,15 @@
             for n in range(needed[b] * cap):
                 slots_a[b + 1][n] = slots_a[b][n]
 
-    middle = cells // 2
+    quarter = cells // 4
     for b in batches:
         grp_wait(*i_args[b])
         second[b] = whole(lambda part: box_i[b, part], b)
         charge = second[b] * shifted[b]
-        left, right = charge[:, :middle], mirrored(charge[:, middle:])
-        field[b, :, :middle] = product(left + right, 0)
-        field[b, :, middle:] = product(left - right, 1)
-        field[b] = along_x(along_x(field[b]) * green)
-        even = product(field[b, :, :middle], 2)
-        odd = product(field[b, :, middle:], 3)
-        field[b, :, :middle] = even + odd
-        field[b, :, middle:] = mirrored(even - odd)
+        spectrum = joined([product(part, 2 * q) for q, part in enumerate(folded(charge))])
+        spectrum = along_x(along_x(spectrum) * green)
+        field[b] = unfolded([
+            product(spectrum[:, q * quarter : (q + 1) * quarter], 2 * q + 1) for q in range(4)])
         code, top = encode(field[b] * shifted[b])
         for part in range(regions):
             term_i[b, part] = code[part * depth : (part + 1) * depth, :]
@@ -401,8 +429,8 @@
     cap = 2 * rows // groups
     length = depth * regions
     vmem = pl.BlockSpec(memory_space=pltpu.VMEM)
-    operands = (pairs, offsets, orbitals, jnp.asarray(fixed_tables(length)))
-    spaces = [pltpu.SMEM, pltpu.SMEM, pltpu.VMEM, pltpu.VMEM]
+    operands = (pairs, offsets, orbitals, *[jnp.asarray(t) for t in fixed_tables(length)])
+    spaces = [pltpu.SMEM, pltpu.SMEM] + [pltpu.VMEM] * 3
     by_slot = (groups, cap, depth, cells)
     by_batch = (share, regions, depth, cells)
     by_region = (regions, depth, cells)
@@ -411,14 +439,14 @@
     _, needed, _ = slot_order(groups, cap, regions, rows)
     parts = [last - first for first, last in zip([0] + needed[:-1], needed)]
     box = (length, cells)
-    table = (4, cells // 2, cells // 2)
     i16 = jnp.int16
     return pl.pallas_call(
         exchange_kernel,
         out_shape=(
-            jax.ShapeDtypeStruct(by_slot, F32), jax.ShapeDtypeStruct((rows, depth, cells), F32)),
+            jax.ShapeDtypeStruct(by_slot, F32), jax.ShapeDtypeStruct((rows, depth, cells), F32),
+            pltpu.SMEM((3, groups * cap), jnp.int32)),
         in_specs=[pl.BlockSpec(memory_space=pltpu.HBM)] * len(operands),
-        out_specs=(vmem, vmem),
+        out_specs=(vmem, vmem, pl.BlockSpec(memory_space=pltpu.SMEM)),
         scratch_shapes=[
             *[space(x.shape, x.dtype) for space, x in zip(spaces, operands)],
             dma((len(operands),)),
@@ -431,7 +459,6 @@
             pltpu.VMEM((regions, share, depth, cells), BF16),
             pltpu.VMEM((share, *box), F32), pltpu.VMEM((share, *box), F32),
             pltpu.VMEM((share, *box), F32),
-            pltpu.VMEM(table, BF16), pltpu.VMEM(table, BF16),
             pltpu.VMEM(by_batch, i16), pltpu.VMEM(by_batch, F32),
             [pltpu.VMEM(by_region, i16) for _ in range(share)],
             [pltpu.VMEM(((b + 1) * regions, depth, cells), i16) for b in range(share)],
@@ -449,43 +476,34 @@
     )(*[pltpu.with_memory_space_constraint(x, pltpu.HBM) for x in operands])
 
 
-def collect_kernel(pairs_in, landed, home, out, pairs, sem_in):
+def collect_kernel(landed, home, targets, out):
     groups, cap = landed.shape[:2]
-    rows = home.shape[0]
-    order, _, _ = slot_order(groups, cap, lax.axis_size("grp"), rows)
-    me = lax.axis_index("orb")
-    load = pltpu.make_async_copy(pairs_in, pairs, sem_in)
-    load.start()
     out[...] = jnp.zeros_like(out)
-    load.wait()
-    for r in range(rows):
-        k = pairs[0, me, r]
-        out[k] += home[r]
+    for r in range(home.shape[0]):
+        out[targets[2, r]] += home[r]
     for n in range(groups):
-        block = partner(me, order[n])
         for c in range(cap):
-            k, valid = find(pairs, block, me * cap + c, lambda r: pairs[1, block, r], rows)
-            out[k] += jnp.where(valid > 0, landed[n, c], 0.0)
-
-
-def collect(pairs, landed, home, shape):
+            slot = n * cap + c
+            out[targets[0, slot]] += jnp.where(targets[1, slot] > 0, landed[n, c], 0.0)
+
+
+def collect(landed, home, targets, shape):
     vmem = pl.BlockSpec(memory_space=pltpu.VMEM)
     return pl.pallas_call(
         collect_kernel,
         out_shape=jax.ShapeDtypeStruct(shape, F32),
-        in_specs=[pl.BlockSpec(memory_space=pltpu.HBM), vmem, vmem],
+        in_specs=[vmem, vmem, pl.BlockSpec(memory_space=pltpu.SMEM)],
         out_specs=vmem,
-        scratch_shapes=[pltpu.SMEM(pairs.shape, pairs.dtype), pltpu.SemaphoreType.DMA],
         compiler_params=pltpu.CompilerParams(vmem_limit_bytes=32 * 1024 * 1024),
-    )(pltpu.with_memory_space_constraint(pairs, pltpu.HBM), landed, home)
+    )(landed, home, pltpu.with_memory_space_constraint(targets, pltpu.SMEM))
 
 
 def per_device(orbitals, pair_list, offsets):
     groups = lax.axis_size("orb")
     regions = lax.axis_size("grp")
     pairs = jnp.transpose(pair_list, (2, 0, 1))
-    landed, home = exchange_terms(pairs, offsets.T, orbitals, groups, regions)
-    return collect(pairs, landed, home, orbitals.shape)
+    landed, home, targets = exchange_terms(pairs, offsets.T, orbitals, groups, regions)
+    return collect(landed, home, targets, orbitals.shape)
 
 
 def solution(mesh):

time: 28.9 us -> 27.1 us (0.938)
  Pallas kernels: 28.6 us -> 26.8 us
    pallas_call x1, Pallas kernels: 26.1 us -> 25.2 us  [exchange_terms(): pl.pallas_call(exchange_kernel, out_shape=(jax.ShapeDtypeStruct(by_slot,...]
    pallas_call x1, Pallas kernels: 2.46 us -> 1.59 us  [collect(): pl.pallas_call(collect_kernel, out_shape=jax.ShapeDtypeStruct(shape, F32)...]
where the time goes in v5:
time: 27.1 us; the launch traced here: 26.8 us
  Pallas kernels  26.8 us (99%)
    pallas_call x1, Pallas kernels, exchange_terms(): pl.pallas_call(exchange_kernel, out_shape=(jax.ShapeDtypeStruct(by_slot,...  25.2 us
    pallas_call x1, Pallas kernels, collect(): pl.pallas_call(collect_kernel, out_shape=jax.ShapeDtypeStruct(shape, F32)...  1.59 us

profile of v5, /device:TPU:0, one launch (start us, length us, event | category | flops | bytes accessed | tf_op | source)
XLA Modules:
  0.0 26.8 jit_solution(2954156358843527047)
XLA Ops:
  0.0 25.2 %shard_map.55 = (f32[8,2,8,1024]{3,2,1,0:T(8,128)S(1)}, f32[8,8,1024]{2,1,0:T(8,128)S(1)}, s32[3,16]{1,0:T(4,128)S(4)}) custom-call(s32[3,8,8]{2,1,0:T(8,128)} %bitcast.2, s32[3,512]{1,0:T(4,128)} %bitcast.3, bf16[64,8,1024]{2,1,0:T(8,128)(2,1)} %orbitals_in.1, bf16[16,256,256]{2,1,0:T(8,128)(2,1)} %constant.4.clone.tables_in, f32[32,1152]{1,0:T(8,128)} %constant.5.clone.small_in), custom_call_target="tpu_custom_call" | custom-call | tf_op jit(solution)/shard_map/pallas_call | solution.py:443
  25.2 1.6 %shard_map.56 = f32[64,8,1024]{2,1,0:T(8,128)} custom-call(f32[8,2,8,1024]{3,2,1,0:T(8,128)S(1)} %get-tuple-element.8.landed, f32[8,8,1024]{2,1,0:T(8,128)S(1)} %get-tuple-element.9.home, s32[3,16]{1,0:T(4,128)S(4)} %get-tuple-element.10.targets), custom_call_target="tpu_custom_call" | custom-call | tf_op jit(solution)/shard_map/pallas_call | solution.py:492

commit v6 on v5

--- a/solution.py
+++ b/solution.py
@@ -62,10 +62,6 @@
     return jnp.dot(left, right, preferred_element_type=F32)
 
 
-def grp_order(count):
-    return sorted(range(1, count), key=lambda k: -min(k, count - k))
-
-
 def slot_order(groups, cap, regions, rows):
     far = list(range(groups))[::-1]
     share = rows // regions
@@ -128,13 +124,13 @@
     local_count = orbitals.shape[0]
     me = lax.axis_index("orb")
     region = lax.axis_index("grp")
-    grp_steps = grp_order(regions)
+    grp_steps = range(regions)[:0:-1]
     order, needed, closed = slot_order(groups, cap, regions, rows)
     batches = range(share)
     begun = []
 
     def grp_peer(k):
-        return lax.rem(region + k, regions)
+        return partner(region, k)
 
     def other(n):
         return partner(me, order[n])
@@ -166,10 +162,18 @@
             send_a[n, c] = orbitals[asked[n * cap + c][0]]
     pl.semaphore_wait(barrier, groups + regions - 2)
 
-    def orb_copy(n, source, target, send_sem, recv_sem):
+    def orb_copy(peer, source, target, send_sem, recv_sem):
         return pltpu.make_async_remote_copy(
             src_ref=source, dst_ref=target, send_sem=send_sem, recv_sem=recv_sem,
-            device_id={"orb": other(n)}, device_id_type=MESH)
+            device_id={"orb": peer}, device_id_type=MESH)
+
+    def pair_places(n):
+        chip = order[n] // 2
+        if chip == 0:
+            return [(n, other(n))]
+        core = lax.rem(me, 2)
+        base = 2 * partner(lax.div(me, 2), chip)
+        return [(n + 1 - core, base), (n + core, base + 1)]
 
     def bytes_of(ref, sem):
         return pltpu.make_async_copy(ref, ref, sem)
@@ -194,13 +198,12 @@
 
     spans = [range(needed[b - 1] if b else 0, needed[b]) for b in batches]
 
-    def box_copy(b, n):
-        return orb_copy(n, send_a.at[n], recv_a[b].at[n - spans[b][0]], sem_sa.at[0], sem_ra.at[b])
-
-    for b in batches:
-        for n in spans[b]:
-            if order[n]:
-                box_copy(b, n).start()
+    for b in batches:
+        for pair in spans[b][::2]:
+            for n, peer in pair_places(pair):
+                orb_copy(
+                    peer, send_a.at[n], recv_a[b].at[n - spans[b][0]], sem_sa.at[0], sem_ra.at[b],
+                ).start()
     begun.append(bytes_of(send_a.at[pl.ds(0, groups - 1)], sem_sa.at[0]))
     places = []
     for r in range(rows):
@@ -226,6 +229,9 @@
 
     row_of = [ranked([jnp.int32(r) for r in range(rows)], q) for q in range(rows)]
     place_of = [ranked(places, q) for q in range(rows)]
+    rank_of = [
+        find(pairs, me, other(n) * cap + c, lambda r: ranks[r], rows)[0]
+        for n in range(groups) for c in range(cap)]
 
     for b in batches:
         for part in range(regions):
@@ -369,12 +375,6 @@
             term_j[b, part] = term[part * depth : (part + 1) * depth, :]
         rows_j[b, region] = term_j[b, region]
 
-    def term_copies(b, n):
-        return (
-            orb_copy(n, send_top.at[n], recv_top.at[n], sem_sw.at[0], sem_rw.at[b]),
-            orb_copy(n, send_d.at[n], recv_d.at[n], sem_sd.at[0], sem_rd.at[n]),
-        )
-
     sends = []
     for b in batches:
         grp_wait(*t_args[b])
@@ -384,18 +384,19 @@
                 every_i[later][b * regions + part] = rows_i[b][part]
                 every_top[later][b * regions + part] = top_rows[b][part]
         leaving = range(closed[b - 1] if b else 0, closed[b])
-        leaving = sorted(leaving, key=lambda n: -order[n])
         for n in leaving:
             for c in range(cap):
-                q, _ = find(pairs, me, other(n) * cap + c, lambda r: ranks[r], rows)
-                q = jnp.minimum(q, (b + 1) * regions - 1)
+                q = jnp.minimum(rank_of[n * cap + c], (b + 1) * regions - 1)
                 send_d[n, c] = every_i[b][q]
                 send_top[n, c : c + 1] = every_top[b][q]
-        for n in leaving:
-            if order[n]:
-                for copy in term_copies(b, n):
-                    copy.start()
-        sends.append([n for n in leaving if order[n]])
+        pairs_leaving = sorted(leaving[::2], key=lambda n: -order[n])
+        for pair in pairs_leaving:
+            for n, peer in pair_places(pair):
+                orb_copy(
+                    peer, send_top.at[n], recv_top.at[n], sem_sw.at[0], sem_rw.at[b]).start()
+                orb_copy(
+                    peer, send_d.at[n], recv_d.at[n], sem_sd.at[0], sem_rd.at[pair // 2]).start()
+        sends.append(pairs_leaving)
         if b == 0:
             for args in u_args:
                 grp_send(*args)
@@ -412,10 +413,12 @@
     for r in range(rows):
         home[r] = rows_j[lax.div(ranks[r], regions), lax.rem(ranks[r], regions)]
     for b in batches:
-        bytes_of(recv_top.at[pl.ds(0, len(sends[b]))], sem_rw.at[b]).wait()
-        for n in sends[b]:
-            bytes_of(recv_d.at[n], sem_rd.at[n]).wait()
-            arrived(n, recv_d, recv_top)
+        away = [[n for n in (pair, pair + 1) if order[n]] for pair in sends[b]]
+        bytes_of(recv_top.at[pl.ds(0, sum(map(len, away)))], sem_rw.at[b]).wait()
+        for pair, both in zip(sends[b], away):
+            bytes_of(recv_d.at[pl.ds(pair, len(both))], sem_rd.at[pair // 2]).wait()
+            for n in both:
+                arrived(n, recv_d, recv_top)
     begun.append(bytes_of(send_top.at[pl.ds(0, groups - 1)], sem_sw.at[0]))
     begun.append(bytes_of(send_d.at[pl.ds(0, groups - 1)], sem_sd.at[0]))
     for copy in begun:
@@ -435,7 +438,7 @@
     by_batch = (share, regions, depth, cells)
     by_region = (regions, depth, cells)
     dma = pltpu.SemaphoreType.DMA
-    one, each, orb_sem = dma((1,)), dma((share,)), dma((groups,))
+    one, each, orb_sem = dma((1,)), dma((share,)), dma((groups // 2,))
     _, needed, _ = slot_order(groups, cap, regions, rows)
     parts = [last - first for first, last in zip([0] + needed[:-1], needed)]
     box = (length, cells)

time: 27.1 us -> 26.2 us (0.967)
  Pallas kernels: 26.8 us -> 25.9 us
    pallas_call x1, Pallas kernels: 25.2 us -> 24.4 us  [exchange_terms(): pl.pallas_call(exchange_kernel, out_shape=(jax.ShapeDtypeStruct(by_slot,...]
where the time goes in v6:
time: 26.2 us; the launch traced here: 26 us
  Pallas kernels  25.9 us (99%)
    pallas_call x1, Pallas kernels, exchange_terms(): pl.pallas_call(exchange_kernel, out_shape=(jax.ShapeDtypeStruct(by_slot,...  24.4 us
    pallas_call x1, Pallas kernels, collect(): pl.pallas_call(collect_kernel, out_shape=jax.ShapeDtypeStruct(shape, F32)...  1.6 us

profile of v6, /device:TPU:0, one launch (start us, length us, event | category | flops | bytes accessed | tf_op | source)
XLA Modules:
  0.0 26.0 jit_solution(15946900503605916924)
XLA Ops:
  0.0 24.4 %shard_map.55 = (f32[8,2,8,1024]{3,2,1,0:T(8,128)S(1)}, f32[8,8,1024]{2,1,0:T(8,128)S(1)}, s32[3,16]{1,0:T(4,128)S(4)}) custom-call(s32[3,8,8]{2,1,0:T(8,128)} %bitcast.2, s32[3,512]{1,0:T(4,128)} %bitcast.3, bf16[64,8,1024]{2,1,0:T(8,128)(2,1)} %orbitals_in.1, bf16[16,256,256]{2,1,0:T(8,128)(2,1)} %constant.4.clone.tables_in, f32[32,1152]{1,0:T(8,128)} %constant.5.clone.small_in), custom_call_target="tpu_custom_call" | custom-call | tf_op jit(solution)/shard_map/pallas_call | solution.py:446
  24.4 1.6 %shard_map.56 = f32[64,8,1024]{2,1,0:T(8,128)} custom-call(f32[8,2,8,1024]{3,2,1,0:T(8,128)S(1)} %get-tuple-element.8.landed, f32[8,8,1024]{2,1,0:T(8,128)S(1)} %get-tuple-element.9.home, s32[3,16]{1,0:T(4,128)S(4)} %get-tuple-element.10.targets), custom_call_target="tpu_custom_call" | custom-call | tf_op jit(solution)/shard_map/pallas_call | solution.py:495

commit v7 on v6

--- a/solution.py
+++ b/solution.py
@@ -141,7 +141,7 @@
             (pairs_in, pairs), (orbitals_in, orbitals), (offsets_in, offsets),
             (tables_in, tables), (small_in, small)))
     ]
-    for load in loads:
+    for load in loads[:2]:
         load.start()
     barrier = pltpu.get_barrier_semaphore()
     for k in range(1, groups):
@@ -154,12 +154,18 @@
     asked = []
     for n in range(groups):
         block = other(n)
+        named = [(pairs[2, block, r] - me * cap, pairs[1, block, r]) for r in range(rows)]
         for c in range(cap):
-            asked.append(find(pairs, block, me * cap + c, lambda r: pairs[1, block, r], rows))
+            local = jnp.int32(0)
+            for slot, place in named:
+                local = jnp.where(slot == c, place, local)
+            asked.append(local)
     loads[1].wait()
+    for load in loads[2:]:
+        load.start()
     for n in range(groups):
         for c in range(cap):
-            send_a[n, c] = orbitals[asked[n * cap + c][0]]
+            send_a[n, c] = orbitals[asked[n * cap + c]]
     pl.semaphore_wait(barrier, groups + regions - 2)
 
     def orb_copy(peer, source, target, send_sem, recv_sem):
@@ -244,9 +250,12 @@
                     recv_a[b][n - spans[b][0], c] = send_a[n, c]
     box_j[region] = stage_j[region]
 
-    for n, (local, valid) in enumerate(asked):
-        targets[0, n] = local
-        targets[1, n] = valid
+    for n in range(groups):
+        for c in range(cap):
+            local, valid = find(
+                pairs, other(n), me * cap + c, lambda r: pairs[1, other(n), r], rows)
+            targets[0, n * cap + c] = local
+            targets[1, n * cap + c] = valid
     for r in range(rows):
         targets[2, r] = pairs[0, me, r]
 
@@ -339,17 +348,21 @@
     for b in batches:
         away = sum(order[n] > 0 for n in spans[b])
         bytes_of(recv_a[b].at[pl.ds(0, away)], sem_ra.at[b]).wait()
-        for n in spans[b]:
-            for c in range(cap):
-                slots_a[b][n * cap + c] = recv_a[b][n - spans[b][0], c]
+        if b:
+            for n in spans[b]:
+                for c in range(cap):
+                    slots_a[b][n * cap + c] = recv_a[b][n - spans[b][0], c]
         for part in range(regions):
             place = jnp.minimum(place_of[b * regions + part], needed[b] * cap - 1)
-            stage_i[b, part] = slots_a[b][place]
+            if b:
+                stage_i[b, part] = slots_a[b][place]
+            else:
+                stage_i[b, part] = recv_a[b][lax.div(place, cap), lax.rem(place, cap)]
         grp_send(*i_args[b])
         box_i[b, region] = stage_i[b, region]
         if b + 1 < share:
             for n in range(needed[b] * cap):
-                slots_a[b + 1][n] = slots_a[b][n]
+                slots_a[b + 1][n] = slots_a[b][n] if b else recv_a[b][n // cap, n % cap]
 
     quarter = cells // 4
     for b in batches:
@@ -379,16 +392,16 @@
     for b in batches:
         grp_wait(*t_args[b])
         grp_wait(*v_args[b])
-        for part in range(regions):
-            for later in range(b, share):
-                every_i[later][b * regions + part] = rows_i[b][part]
-                every_top[later][b * regions + part] = top_rows[b][part]
+        if b:
+            for part in range(regions):
+                every_i[b][b * regions + part] = rows_i[b][part]
+                every_top[b][b * regions + part] = top_rows[b][part]
         leaving = range(closed[b - 1] if b else 0, closed[b])
         for n in leaving:
             for c in range(cap):
                 q = jnp.minimum(rank_of[n * cap + c], (b + 1) * regions - 1)
-                send_d[n, c] = every_i[b][q]
-                send_top[n, c : c + 1] = every_top[b][q]
+                send_d[n, c] = every_i[b][q] if b else rows_i[b][q]
+                send_top[n, c : c + 1] = every_top[b][q] if b else top_rows[b][q]
         pairs_leaving = sorted(leaving[::2], key=lambda n: -order[n])
         for pair in pairs_leaving:
             for n, peer in pair_places(pair):
@@ -397,6 +410,10 @@
                 orb_copy(
                     peer, send_d.at[n], recv_d.at[n], sem_sd.at[0], sem_rd.at[pair // 2]).start()
         sends.append(pairs_leaving)
+        for later in range(b + 1, share):
+            for part in range(regions):
+                every_i[later][b * regions + part] = rows_i[b][part]
+                every_top[later][b * regions + part] = top_rows[b][part]
         if b == 0:
             for args in u_args:
                 grp_send(*args)

time: 26.2 us -> 26.2 us (level)
  no operation moved by 1% of the time
where the time goes in v7:
time: 26.2 us; the launch traced here: 25.9 us
  Pallas kernels  25.9 us (99%)
    pallas_call x1, Pallas kernels, exchange_terms(): pl.pallas_call(exchange_kernel, out_shape=(jax.ShapeDtypeStruct(by_slot,...  24.3 us
    pallas_call x1, Pallas kernels, collect(): pl.pallas_call(collect_kernel, out_shape=jax.ShapeDtypeStruct(shape, F32)...  1.59 us

profile of v7, /device:TPU:0, one launch (start us, length us, event | category | flops | bytes accessed | tf_op | source)
XLA Modules:
  0.0 25.9 jit_solution(6998132809264163130)
XLA Ops:
  0.0 24.3 %shard_map.55 = (f32[8,2,8,1024]{3,2,1,0:T(8,128)S(1)}, f32[8,8,1024]{2,1,0:T(8,128)S(1)}, s32[3,16]{1,0:T(4,128)S(4)}) custom-call(s32[3,8,8]{2,1,0:T(8,128)} %bitcast.2, s32[3,512]{1,0:T(4,128)} %bitcast.3, bf16[64,8,1024]{2,1,0:T(8,128)(2,1)} %orbitals_in.1, bf16[16,256,256]{2,1,0:T(8,128)(2,1)} %constant.4.clone.tables_in, f32[32,1152]{1,0:T(8,128)} %constant.5.clone.small_in), custom_call_target="tpu_custom_call" | custom-call | tf_op jit(solution)/shard_map/pallas_call | solution.py:463
  24.3 1.6 %shard_map.56 = f32[64,8,1024]{2,1,0:T(8,128)} custom-call(f32[8,2,8,1024]{3,2,1,0:T(8,128)S(1)} %get-tuple-element.8.landed, f32[8,8,1024]{2,1,0:T(8,128)S(1)} %get-tuple-element.9.home, s32[3,16]{1,0:T(4,128)S(4)} %get-tuple-element.10.targets), custom_call_target="tpu_custom_call" | custom-call | tf_op jit(solution)/shard_map/pallas_call | solution.py:512
